TPU v7x, 128 devices: a whole 4x4x4 slice. The times are simulated.
128 devices in a mesh: row: 8 (over z, core), col: 16 (over x, y).
Axes of the slice: x: 4, y: 4, z: 4, core: 2. Of those that a mesh axis runs over, the one named last changes fastest.
Arguments:
- grad_terms: bfloat16 [16, 2, 4096, 10240], P('col', None, 'row'), may hold values from -25 to 25, as said below
- row_moment: float32 [2, 4096], P(None, 'row'), may hold values from 0.01 to 3
- col_moment: float32 [2, 10240], P(None, 'col'), may hold values from 0.01 to 1
Outputs:
- update: float32 [2, 4096, 10240], P(None, 'row', 'col')
- new_rows: float32 [2, 4096], P(None, 'row')
- new_cols: float32 [2, 10240], P(None, 'col')
Inputs may be any that keep to these rules, and one draw needn't show every extreme that they name: `grad_terms`: partial gradient terms of the 16 batch shards.
All inputs are finite; a program needn't handle non-finite values.
Results may differ from a plain program's by a relative error of at most 0.0003.
Values sent between devices are 32-bit elements; how exact they have to be, the bound alone decides.
A program may use at most 256 MiB of HBM per device.

v0:
```python
import jax
import jax.numpy as jnp
from jax import lax
from jax.sharding import Mesh
from jax.sharding import PartitionSpec as P

D = 4096
FF = 10240
COL = ("col_0", "col_1")
ROW = ("row_0", "row_1")
ROW_COL = ("row_0", "row_1", "col_0", "col_1")


second_decay = 1.0 - 100.0 ** (-0.8)
tiny_square = 1e-30


def by_axis(value, axes):
    for axis in axes:
        value = lax.psum(value, axis)
    return value


def from_everyone(value, axis):
    length = lax.axis_size(axis)
    return lax.all_to_all(
        jnp.broadcast_to(value[None], (length, *value.shape)), axis, 0, 0, tiled=True
    )


def taken_together(value, axis):
    everything = from_everyone(value, axis)
    return jnp.sum(everything, axis=0)


def on_device(grad_terms, row_moment, col_moment):
    partial_terms = grad_terms[0]
    gradient = lax.psum_scatter(
        partial_terms.astype(jnp.float32), COL, scatter_dimension=2, tiled=True
    )
    squares = gradient * gradient + tiny_square
    row_part = jnp.sum(squares, axis=2)
    col_part = jnp.sum(squares, axis=1)
    row_full = by_axis(row_part, COL)
    col_full = taken_together(col_part, ROW)
    new_rows = second_decay * row_moment + (1.0 - second_decay) * row_full / FF
    new_cols = second_decay * col_moment + (1.0 - second_decay) * col_full / D
    row_level = taken_together(jnp.sum(new_rows, axis=1), ROW) / D
    estimate = new_rows[:, :, None] * new_cols[:, None, :] / row_level[:, None, None]
    raw_update = gradient / jnp.sqrt(estimate)
    clip_total = by_axis(jnp.sum(raw_update * raw_update, axis=(1, 2)), ROW_COL)
    clip_scale = jnp.maximum(1.0, jnp.sqrt(clip_total / (D * FF)))
    update = raw_update / clip_scale[:, None, None]
    return (update, new_rows, new_cols)


def solution(mesh):
    torus = Mesh(mesh.devices.reshape(4, 2, 4, 4), ("row_0", "row_1", "col_0", "col_1"))
    in_specs = (P(COL, None, ROW, None), P(None, ROW), P(None, COL))
    out_specs = (P(None, ROW, COL), P(None, ROW), P(None, COL))
    return jax.shard_map(
        on_device, mesh=torus, in_specs=in_specs, out_specs=out_specs, check_vma=False
    )
```

profile of v0, /device:TPU:1, one launch (start us, length us, event | category | flops | bytes accessed | tf_op | source)
XLA Modules:
  0.0 345.5 jit_solution(865920876376698171)
XLA Ops:
  7.2 0.0 reduce-scatter.2.cloned.1.call-start
  7.2 23.1 %bitcast_convert_fusion = f32[2,512,10240]{2,1,0:T(8,128)} fusion(bf16[1,2,512,10240]{3,2,1,0:T(8,128)(2,1)} %param.3), kind=kLoop, calls=%fused_computation | loop fusion | flops 10485760 | bytes 62914560 | tf_op jit(solution)/shard_map/convert_element_type | solution.py:39
  30.3 0.0 reduce-scatter.2.cloned.1.call-update
  30.3 0.0 copy-start.4
  30.3 0.0 copy-start.3
  30.3 240.1 %reduce-scatter.2.cloned.1.call-done = f32[2,512,640]{2,1,0:T(8,128)} async-done(((f32[2,512,10240]{2,1,0:T(8,128)}), f32[2,512,640]{2,1,0:T(8,128)}) %reduce-scatter.2.cloned.1.call-update) | async-done | bytes 2621456 | tf_op jit(solution)/shard_map/reduce_scatter | solution.py:38
  270.4 2.4 fusion
  272.8 8.5 %psum.42 = f32[2,512]{1,0:T(2,128)S(1)} all-reduce(f32[2,512]{1,0:T(2,128)S(1)} %get-tuple-element.4), channel_id=1, replica_groups=mesh['row_0'=4,'row_1'=2,'col_0'=4,'col_1'=4] {'col_0'}, use_global_device_ids=true, to_apply=%region_2.0 | all-reduce | flops 1024 | bytes 8192 | tf_op jit(solution)/shard_map/psum | solution.py:20
  281.4 6.5 %psum.43 = f32[2,512]{1,0:T(2,128)S(1)} all-reduce(f32[2,512]{1,0:T(2,128)S(1)} %psum.42), channel_id=1, replica_groups=mesh['row_0'=4,'row_1'=2,'col_0'=4,'col_1'=4] {'col_1'}, use_global_device_ids=true, to_apply=%region_3.0 | all-reduce | flops 1024 | bytes 8192 | tf_op jit(solution)/shard_map/psum | solution.py:20
  287.9 0.0 copy-done.4
  287.9 0.1 fusion.2
  288.0 13.6 %all_to_all.11 = f32[8,1,2]{2,1,0:T(1,128)S(1)} all-to-all(f32[8,1,2]{2,1,0:T(1,128)S(1)} %broadcast_in_dim.5), channel_id=1, replica_groups=mesh['row_0'=4,'row_1'=2,'col_0'=4,'col_1'=4] {'row_0','row_1'}, dimensions={0} | all-to-all | bytes 128 | tf_op jit(solution)/shard_map/all_to_all | solution.py:26
  301.6 0.6 broadcast_in_dim.4
  302.3 3.9 %all-to-all-start = ((f32[8,2,640]{2,1,0:T(2,128)}), f32[8,2,640]{2,1,0:T(2,128)S(1)}, u32[]{:S(2)}, u32[]{:S(2)}) async-start(f32[8,2,640]{2,1,0:T(2,128)} %broadcast_in_dim.4), calls=%async_computation.1 | async-start | bytes 81920 | tf_op jit(solution)/shard_map/all_to_all | solution.py:26
  306.2 4.7 %all-to-all-done = f32[8,2,640]{2,1,0:T(2,128)S(1)} async-done(((f32[8,2,640]{2,1,0:T(2,128)}), f32[8,2,640]{2,1,0:T(2,128)S(1)}, u32[]{:S(2)}, u32[]{:S(2)}) %all-to-all-start) | async-done | bytes 40992 | tf_op jit(solution)/shard_map/all_to_all | solution.py:26
  311.0 0.0 copy-done.3
  311.0 0.0 copy-start.1
  311.0 0.0 copy-done
  311.1 0.9 multiply_reduce_fusion
  311.9 6.8 %psum.44 = f32[2]{0:T(128)S(1)} all-reduce(f32[2]{0:T(128)S(1)} %multiply_reduce_fusion), channel_id=1, replica_groups=mesh['row_0'=4,'row_1'=2,'col_0'=4,'col_1'=4] {'row_0'}, use_global_device_ids=true, to_apply=%region_9.0 | all-reduce | flops 2 | bytes 16 | tf_op jit(solution)/shard_map/psum | solution.py:20
  318.8 4.9 %psum.45 = f32[2]{0:T(128)S(1)} all-reduce(f32[2]{0:T(128)S(1)} %psum.44), channel_id=1, replica_groups=mesh['row_0'=4,'row_1'=2,'col_0'=4,'col_1'=4] {'row_1'}, use_global_device_ids=true, to_apply=%region_10.0 | all-reduce | flops 2 | bytes 16 | tf_op jit(solution)/shard_map/psum | solution.py:20
  323.6 6.9 %psum.46 = f32[2]{0:T(128)S(1)} all-reduce(f32[2]{0:T(128)S(1)} %psum.45), channel_id=1, replica_groups=mesh['row_0'=4,'row_1'=2,'col_0'=4,'col_1'=4] {'col_0'}, use_global_device_ids=true, to_apply=%region_11.0 | all-reduce | flops 2 | bytes 16 | tf_op jit(solution)/shard_map/psum | solution.py:20
  330.5 6.1 %psum.47 = f32[2]{0:T(128)S(1)} all-reduce(f32[2]{0:T(128)S(1)} %psum.46), channel_id=1, replica_groups=mesh['row_0'=4,'row_1'=2,'col_0'=4,'col_1'=4] {'col_1'}, use_global_device_ids=true, to_apply=%region_12.0 | all-reduce | flops 2 | bytes 16 | tf_op jit(solution)/shard_map/psum | solution.py:20
  336.6 2.0 broadcast_divide_fusion
  (10 shorter events, 0.1 us)
Async XLA Ops:
  7.2 263.3 %reduce-scatter.2.cloned.1.call-start = ((), (), s32[]{:S(2)}) async-start(), calls=%async_computation.3 | async-start | bytes 44564480 | tf_op jit(solution)/shard_map/reduce_scatter | solution.py:38
  30.3 257.6 %copy-start.4 = (f32[2,512]{1,0:T(2,128)S(1)}, f32[2,512]{1,0:T(2,128)}, u32[]{:S(2)}) copy-start(f32[2,512]{1,0:T(2,128)} %param.4) | copy-start | bytes 12292
  30.3 280.7 %copy-start.3 = (f32[2,640]{1,0:T(2,128)S(1)}, f32[2,640]{1,0:T(2,128)}, u32[]{:S(2)}) copy-start(f32[2,640]{1,0:T(2,128)} %param.5) | copy-start | bytes 15364
  270.4 40.6 %copy-start = (f32[2,512,640]{2,1,0:T(8,128)S(1)}, f32[2,512,640]{2,1,0:T(8,128)}, u32[]{:S(2)}) copy-start(f32[2,512,640]{2,1,0:T(8,128)} %reduce-scatter.2.cloned.1.call-done) | copy-start | bytes 7864324
  288.0 50.6 %copy-start.2 = (f32[2,512]{1,0:T(2,128)}, f32[2,512]{1,0:T(2,128)S(1)}, u32[]{:S(2)}) copy-start(f32[2,512]{1,0:T(2,128)S(1)} %get-tuple-element.6) | copy-start | bytes 12292
  302.3 8.7 %all-to-all-start = ((f32[8,2,640]{2,1,0:T(2,128)}), f32[8,2,640]{2,1,0:T(2,128)S(1)}, u32[]{:S(2)}, u32[]{:S(2)}) async-start(f32[8,2,640]{2,1,0:T(2,128)} %broadcast_in_dim.4), calls=%async_computation.1 | async-start | bytes 81920 | tf_op jit(solution)/shard_map/all_to_all | solution.py:26
  311.0 27.6 %copy-start.1 = (f32[2,640]{1,0:T(2,128)}, f32[2,640]{1,0:T(2,128)S(1)}, u32[]{:S(2)}) copy-start(f32[2,640]{1,0:T(2,128)S(1)} %multiply_add_fusion.1) | copy-start | bytes 15364
Sparse Core Ops, SparseCore 0:
  30.4 239.9 reduce-scatter.1
where the time goes:
time: 349 us; the launch traced here: 345 us
  waiting for transfers between devices  245 us (70%)
  blocking collectives  53.3 us (15%)
  other arithmetic  28.5 us (8%)
  between operations  14.1 us (4%)
  starting transfers between devices  3.98 us (1%)
    reduce_scatter x1, waiting for transfers between devices, on_device(): lax.psum_scatter(partial_terms.astype(jnp.float32), COL, scatter_dimensio...  240 us
    psum x6, blocking collectives, by_axis(): value = lax.psum(value, axis)  39.7 us
    convert_element_type x1, other arithmetic, on_device(): partial_terms.astype(jnp.float32)  23.1 us
    all_to_all x1, blocking collectives, from_everyone(): lax.all_to_all(jnp.broadcast_to(value[None], (length, *value.shape)), axi...  13.6 us
  transfers between devices with their start and end apart: 2, of which 2 were waited for; matrix products, arithmetic and copies ran while one was open for 0% of the time, Pallas kernels for 0%

commit v1 on v0

v1 whole, which is shorter than its diff:
```python
import functools

import jax
import jax.numpy as jnp
from jax import lax
from jax.experimental import pallas as pl
from jax.experimental.pallas import tpu as pltpu
from jax.sharding import Mesh
from jax.sharding import PartitionSpec as P

MESH = pl.DeviceIdType.MESH
COL = ("col_0", "col_1")
ROW = ("row_0", "row_1")
RING = 4
LANES = 128
HALF = 8
CHUNK = 2 * HALF
X_SLOTS = 6
X_AHEAD = 3
S_SLOTS = 4

second_decay = 1.0 - 100.0 ** (-0.8)
tiny_square = 1e-30


def wait_bytes(ref, sem):
    pltpu.make_async_copy(ref, ref, sem).wait()


def kernel(
    grad_hbm,
    row_moment,
    col_moment,
    update,
    new_rows,
    new_cols,
    x_in,
    stage,
    land1,
    sum1,
    land2,
    sum2,
    grad,
    row_part,
    col_part,
    row_scale,
    row_land,
    col_land,
    all_land,
    fin_land,
    x_sem,
    send0,
    send1,
    send2,
    send3,
    recv1,
    recv2,
    recv3,
    recv4,
    stat_send,
    stat_recv,
):
    mats, rows = row_moment.shape
    width = col_moment.shape[1]
    block = RING * width
    row_groups = rows // LANES
    n_row0, n_row1 = lax.axis_size("row_0"), lax.axis_size("row_1")
    n_row, n_col = n_row0 * n_row1, RING * RING
    total_rows = n_row * rows
    total_cols = n_col * width
    per_mat = rows // (2 * CHUNK)
    chunks = mats * per_mat

    here = (lax.axis_index("col_0"), lax.axis_index("col_1"))
    my_col = here[0] * RING + here[1]
    my_row = lax.axis_index("row_0") * n_row1 + lax.axis_index("row_1")

    def at(axis, step):
        return lax.rem(here[axis] + (step + RING), RING)

    def neighbour(axis, step):
        return {COL[axis]: at(axis, step)}

    def col_peer(d):
        t = lax.rem(my_col + d, n_col)
        return {"col_0": t // RING, "col_1": lax.rem(t, RING)}

    def row_peer(d):
        t = lax.rem(my_row + d, n_row)
        return {"row_0": t // n_row1, "row_1": lax.rem(t, n_row1)}

    def send(src, dst, s_sem, r_sem, device):
        pltpu.make_async_remote_copy(
            src_ref=src,
            dst_ref=dst,
            send_sem=s_sem,
            recv_sem=r_sem,
            device_id=device,
            device_id_type=MESH,
        ).start()

    def load(k):
        slot = lax.rem(k, X_SLOTS)
        m = k // per_mat
        r = pl.multiple_of(lax.rem(k, per_mat) * (2 * CHUNK), 2 * CHUNK)
        return pltpu.make_async_copy(
            grad_hbm.at[0, m, pl.ds(r, 2 * CHUNK), :], x_in.at[slot], x_sem.at[slot]
        )

    def own(color, k, idx, seg):
        outer, inner = (idx, seg) if color == 0 else (seg, idx)
        c = pl.multiple_of(outer * block + inner * width, LANES)
        v = x_in[
            lax.rem(k, X_SLOTS), color * CHUNK : (color + 1) * CHUNK, pl.ds(c, width)
        ]
        v = v.astype(jnp.float32)
        return v[:HALF], v[HALF:]

    def cols(s):
        return slice(s * width, (s + 1) * width)

    def inner_cols(idx):
        return pl.ds(pl.multiple_of(idx * width, LANES), width)

    def prepare(k):
        slot = lax.rem(k, S_SLOTS)
        load(k).wait()
        for color in range(2):

            @pl.when(k >= S_SLOTS)
            def _():
                wait_bytes(stage.at[slot, color], send0.at[slot, color])

            axis = color
            for s in range(RING):
                top, low = own(color, k, at(axis, 2), s)
                stage[slot, color, 0, :, cols(s)] = top
                stage[slot, color, 1, :, cols(s)] = low
            for s in range(RING):
                _, low = own(color, k, at(axis, 1), s)
                stage[slot, color, 2, :, cols(s)] = low
                top, _ = own(color, k, at(axis, -1), s)
                stage[slot, color, 3, :, cols(s)] = top

    def stage0(k):
        slot = lax.rem(k, S_SLOTS)
        for which, step, land in ((0, 1, 0), (1, -1, 1)):
            for color in range(2):
                send(
                    stage.at[slot, color, which],
                    land1.at[k, color, land],
                    send0.at[slot, color],
                    recv1.at[k, color],
                    neighbour(color, step),
                )
        for which, step in ((2, 1), (3, -1)):
            for color in range(2):
                send(
                    stage.at[slot, color, which],
                    sum1.at[k, color, which],
                    send0.at[slot, color],
                    recv2.at[k, color],
                    neighbour(color, step),
                )

    def stage1(k):
        slot = lax.rem(k, S_SLOTS)
        for color in range(2):
            axis = color
            wait_bytes(land1.at[k, color], recv1.at[k, color])

            @pl.when(k >= S_SLOTS)
            def _():
                wait_bytes(land1.at[k, color], send1.at[slot, color])

            for s in range(RING):
                top, _ = own(color, k, at(axis, 1), s)
                land1[k, color, 0, :, cols(s)] = land1[k, color, 0, :, cols(s)] + top
                _, low = own(color, k, at(axis, -1), s)
                land1[k, color, 1, :, cols(s)] = land1[k, color, 1, :, cols(s)] + low
            for which, step in ((0, 1), (1, -1)):
                send(
                    land1.at[k, color, which],
                    sum1.at[k, color, which],
                    send1.at[slot, color],
                    recv2.at[k, color],
                    neighbour(axis, step),
                )

    def stage2(k):
        slot = lax.rem(k, S_SLOTS)
        for color in range(2):
            axis = color
            wait_bytes(sum1.at[k, color], recv2.at[k, color])

            @pl.when(k >= S_SLOTS)
            def _():
                wait_bytes(sum2.at[k, color], send2.at[slot, color])

            for s in range(RING):
                top, low = own(color, k, at(axis, 0), s)
                sum1[k, color, 0, :, cols(s)] = (
                    sum1[k, color, 0, :, cols(s)]
                    + sum1[k, color, 3, :, cols(s)]
                    + top
                )
                sum1[k, color, 1, :, cols(s)] = (
                    sum1[k, color, 1, :, cols(s)]
                    + sum1[k, color, 2, :, cols(s)]
                    + low
                )
            axis = 1 - color
            for which, step in ((0, 1), (1, -1)):
                send(
                    sum1.at[k, color, which, :, inner_cols(at(axis, 2))],
                    land2.at[k, color, which],
                    send2.at[slot, color],
                    recv3.at[k, color],
                    neighbour(axis, step),
                )
            for half, which, step in ((1, 2, 1), (0, 3, -1)):
                send(
                    sum1.at[k, color, half, :, inner_cols(at(axis, step))],
                    sum2.at[k, color, which],
                    send2.at[slot, color],
                    recv4.at[k, color],
                    neighbour(axis, step),
                )

    def stage3(k):
        slot = lax.rem(k, S_SLOTS)
        for color in range(2):
            axis = 1 - color
            wait_bytes(land2.at[k, color], recv3.at[k, color])

            @pl.when(k >= S_SLOTS)
            def _():
                wait_bytes(land2.at[k, color], send3.at[slot, color])

            for which, step in ((0, 1), (1, -1)):
                land2[k, color, which] = (
                    land2[k, color, which]
                    + sum1[k, color, which, :, inner_cols(at(axis, step))]
                )
                send(
                    land2.at[k, color, which],
                    sum2.at[k, color, which],
                    send3.at[slot, color],
                    recv4.at[k, color],
                    neighbour(axis, step),
                )

    def lane_tiles(v):
        out = v[:, :LANES]
        for c in range(1, width // LANES):
            out = out + v[:, c * LANES : (c + 1) * LANES]
        return out

    def stage4(k):
        m = k // per_mat
        r = lax.rem(k, per_mat) * (2 * CHUNK)
        squares_sum = col_part[m]
        for color in range(2):
            axis = 1 - color
            wait_bytes(sum2.at[k, color], recv4.at[k, color])
            for half, other in ((0, 3), (1, 2)):
                g = (
                    sum2[k, color, half]
                    + sum2[k, color, other]
                    + sum1[k, color, half, :, inner_cols(at(axis, 0))]
                )
                here_rows = pl.ds(
                    pl.multiple_of(r + color * CHUNK + half * HALF, HALF), HALF
                )
                grad[m, here_rows, :] = g
                squares = g * g + tiny_square
                row_part[m, here_rows, :] = lane_tiles(squares)
                squares_sum = squares_sum + squares
        col_part[m] = squares_sum

    def pick(ref, m, lanes):
        return jnp.where(m == 0, ref[0:1, lanes], ref[1:2, lanes])

    def put(ref, m, lanes, value):
        for i in range(mats):

            @pl.when(m == i)
            def _():
                ref[i : i + 1, lanes] = value

    def all_cols(m, buf, which):
        mine = buf.at[m, my_col]

        def one(d, _):
            send(mine, mine, stat_send.at[m, which], stat_recv.at[m, which], col_peer(d))
            return 0

        lax.fori_loop(1, n_col, one, 0)

    def all_rows(m, buf, which):
        mine = buf.at[m, my_row]

        def one(d, _):
            send(mine, mine, stat_send.at[m, which], stat_recv.at[m, which], row_peer(d))
            return 0

        lax.fori_loop(1, n_row, one, 0)

    def wait_all(m, buf, which, n):
        if n > 1:
            wait_bytes(buf.at[m, pl.ds(0, n - 1)], stat_recv.at[m, which])

    def wait_sent(m, buf, which, n):
        if n > 1:
            wait_bytes(buf.at[m, pl.ds(0, n - 1)], stat_send.at[m, which])

    def statistics1(m):
        for b in range(row_groups):
            part = row_part[m, b * LANES : (b + 1) * LANES, :]
            row_land[m, my_col, b : b + 1, :] = jnp.sum(part.T, axis=0, keepdims=True)
        col_land[m, my_row] = jnp.sum(col_part[m], axis=0, keepdims=True)
        all_cols(m, row_land, 0)
        all_rows(m, col_land, 1)

    def statistics2(m):
        wait_all(m, row_land, 0, n_col)
        wait_all(m, col_land, 1, n_row)
        full = row_land[m, 0]
        for s in range(1, n_col):
            full = full + row_land[m, s]
        moments = []
        for b in range(row_groups):
            moment = (
                second_decay * pick(row_moment, m, slice(b * LANES, (b + 1) * LANES))
                + (1.0 - second_decay) * full[b : b + 1] / total_cols
            )
            put(new_rows, m, slice(b * LANES, (b + 1) * LANES), moment)
            moments.append(moment)
            row_scale[b * LANES : (b + 1) * LANES, :] = jnp.broadcast_to(
                lax.rsqrt(moment), (LANES, LANES)
            ).T
        full = col_land[m, 0]
        for s in range(1, n_row):
            full = full + col_land[m, s]
        col = (
            second_decay * pick(col_moment, m, slice(None))
            + (1.0 - second_decay) * full / total_rows
        )
        put(new_cols, m, slice(None), col)
        col_scale = jnp.broadcast_to(lax.rsqrt(col), (HALF, width))

        def rescale(t, total):
            r = pl.ds(pl.multiple_of(t * HALF, HALF), HALF)
            scale = row_scale[r, :]
            for c in range(width // LANES):
                lanes = slice(c * LANES, (c + 1) * LANES)
                v = grad[m, r, lanes] * col_scale[:, lanes] * scale
                update[m, r, lanes] = v
                total = total + v * v
            return total

        total = lax.fori_loop(
            0, rows // HALF, rescale, jnp.zeros((HALF, LANES), jnp.float32)
        )
        level = moments[0]
        for moment in moments[1:]:
            level = level + moment
        all_land[m, my_col] = total
        fin_land[m, my_row, HALF : HALF + 1, :] = level
        all_cols(m, all_land, 2)

    def statistics3(m):
        wait_all(m, all_land, 2, n_col)
        total = all_land[m, 0]
        for s in range(1, n_col):
            total = total + all_land[m, s]
        fin_land[m, my_row, :HALF, :] = total
        all_rows(m, fin_land, 3)

    def statistics4(m):
        wait_all(m, fin_land, 3, n_row)
        total = fin_land[m, 0]
        for s in range(1, n_row):
            total = total + fin_land[m, s]
        level = jnp.sum(total[HALF : HALF + 1], axis=1, keepdims=True) / total_rows
        clip = jnp.sum(
            jnp.sum(total[:HALF], axis=0, keepdims=True), axis=1, keepdims=True
        )
        clip_scale = jnp.maximum(
            1.0, jnp.sqrt(clip * level / (total_rows * total_cols))
        )
        factor = jnp.broadcast_to(jnp.sqrt(level) / clip_scale, (HALF, width))

        def finish(t, _):
            r = pl.ds(pl.multiple_of(t * HALF, HALF), HALF)
            update[m, r, :] = update[m, r, :] * factor
            return 0

        lax.fori_loop(0, rows // HALF, finish, 0)
        wait_sent(m, row_land, 0, n_col)
        wait_sent(m, col_land, 1, n_row)
        wait_sent(m, all_land, 2, n_col)
        wait_sent(m, fin_land, 3, n_row)

    barrier = pltpu.get_barrier_semaphore()

    def greet_col(d, _):
        pl.semaphore_signal(
            barrier, inc=1, device_id=col_peer(d), device_id_type=MESH
        )
        return 0

    def greet_row(d, _):
        pl.semaphore_signal(
            barrier, inc=1, device_id=row_peer(d), device_id_type=MESH
        )
        return 0

    for k in range(X_AHEAD):
        load(k).start()
    lax.fori_loop(1, n_col, greet_col, 0)
    lax.fori_loop(1, n_row, greet_row, 0)
    col_part[...] = jnp.zeros_like(col_part)
    fin_land[...] = jnp.zeros_like(fin_land)
    prepare(0)
    pl.semaphore_wait(barrier, n_col - 1 + n_row - 1)

    def step(it, _):
        @pl.when(it < chunks)
        def _():
            stage0(it)

            @pl.when(it + X_AHEAD < chunks)
            def _():
                load(it + X_AHEAD).start()

        for lag, work in ((1, stage1), (2, stage2), (3, stage3), (4, stage4)):

            @pl.when((it >= lag) & (it < chunks + lag))
            def _():
                work(it - lag)

        @pl.when(it + 1 < chunks)
        def _():
            prepare(it + 1)

        for when, work in (
            ((per_mat + 3, chunks + 3), statistics1),
            ((per_mat + 5, chunks + 4), statistics2),
            ((per_mat + 7, chunks + 5), statistics3),
            ((per_mat + 9, chunks + 6), statistics4),
        ):

            @pl.when((it == when[0]) | (it == when[1]))
            def _():
                work(jnp.where(it == when[0], 0, 1))

        return 0

    lax.fori_loop(0, chunks + 7, step, 0)

    def drain(slot, _):
        for color in range(2):
            wait_bytes(stage.at[slot, color], send0.at[slot, color])
            wait_bytes(land1.at[0, color], send1.at[slot, color])
            wait_bytes(sum2.at[0, color], send2.at[slot, color])
            wait_bytes(land2.at[0, color], send3.at[slot, color])
        return 0

    lax.fori_loop(0, S_SLOTS, drain, 0)


def on_device(grad_terms, row_moment, col_moment):
    _, mats, rows, _ = grad_terms.shape
    width = col_moment.shape[1]
    n_row = lax.axis_size("row_0") * lax.axis_size("row_1")
    n_col = RING * RING
    chunks = mats * rows // (2 * CHUNK)
    f32 = jnp.float32
    vmem = pl.BlockSpec(memory_space=pltpu.VMEM)
    dma = pltpu.SemaphoreType.DMA
    return pl.pallas_call(
        kernel,
        out_shape=(
            jax.ShapeDtypeStruct((mats, rows, width), f32),
            jax.ShapeDtypeStruct((mats, rows), f32),
            jax.ShapeDtypeStruct((mats, width), f32),
        ),
        in_specs=[pl.BlockSpec(memory_space=pl.ANY), vmem, vmem],
        out_specs=(vmem, vmem, vmem),
        scratch_shapes=[
            pltpu.VMEM((X_SLOTS, 2 * CHUNK, n_col * width), jnp.bfloat16),
            pltpu.VMEM((S_SLOTS, 2, 4, HALF, RING * width), f32),
            pltpu.VMEM((chunks, 2, 2, HALF, RING * width), f32),
            pltpu.VMEM((chunks, 2, 4, HALF, RING * width), f32),
            pltpu.VMEM((chunks, 2, 2, HALF, width), f32),
            pltpu.VMEM((chunks, 2, 4, HALF, width), f32),
            pltpu.VMEM((mats, rows, width), f32),
            pltpu.VMEM((mats, rows, LANES), f32),
            pltpu.VMEM((mats, HALF, width), f32),
            pltpu.VMEM((rows, LANES), f32),
            pltpu.VMEM((mats, n_col, rows // LANES, LANES), f32),
            pltpu.VMEM((mats, n_row, 1, width), f32),
            pltpu.VMEM((mats, n_col, HALF, LANES), f32),
            pltpu.VMEM((mats, n_row, 2 * HALF, LANES), f32),
            dma((X_SLOTS,)),
            dma((S_SLOTS, 2)),
            dma((S_SLOTS, 2)),
            dma((S_SLOTS, 2)),
            dma((S_SLOTS, 2)),
            dma((chunks, 2)),
            dma((chunks, 2)),
            dma((chunks, 2)),
            dma((chunks, 2)),
            dma((mats, 4)),
            dma((mats, 4)),
        ],
        compiler_params=pltpu.CompilerParams(
            collective_id=0,
            has_side_effects=True,
            vmem_limit_bytes=60 * 1024 * 1024,
        ),
    )(grad_terms, row_moment, col_moment)


def solution(mesh):
    n_row = mesh.shape["row"]
    core = 2 if n_row > 1 else 1
    torus = Mesh(
        mesh.devices.reshape(n_row // core, core, RING, RING), ROW + COL
    )
    in_specs = (P(COL, None, ROW, None), P(None, ROW), P(None, COL))
    out_specs = (P(None, ROW, COL), P(None, ROW), P(None, COL))
    return jax.shard_map(
        on_device, mesh=torus, in_specs=in_specs, out_specs=out_specs, check_vma=False
    )
```

time: 349 us -> 252 us (0.72); the launches traced: 345 us -> 252 us
  Pallas kernels: 0 us -> 247 us
  waiting for transfers between devices: 245 us -> 0 us
  blocking collectives: 53.3 us -> 0 us
  other arithmetic: 28.5 us -> 0 us
  between operations: 14.1 us -> 0.66 us
  starting transfers between devices: 3.98 us -> 0 us
  local copies, waits for them, and re-layouts: 0.66 us -> 4.6 us
    pallas_call x0 -> x1, Pallas kernels: none -> 247 us  [on_device(): pl.pallas_call(kernel, out_shape=(jax.ShapeDtypeStruct((mats, rows, width...]
    reduce_scatter x1 -> x0, waiting for transfers between devices: 240 us -> none  [on_device(): lax.psum_scatter(partial_terms.astype(jnp.float32), COL, scatter_dimensio...]
    psum x6 -> x0, blocking collectives: 39.7 us -> none  [by_axis(): value = lax.psum(value, axis)]
    convert_element_type x1 -> x0, other arithmetic: 23.1 us -> none  [on_device(): partial_terms.astype(jnp.float32)]
    all_to_all x1 -> x0, blocking collectives: 13.6 us -> none  [from_everyone(): lax.all_to_all(jnp.broadcast_to(value[None], (length, *value.shape)), axi...]
    all_to_all x1 -> x0, waiting for transfers between devices: 4.74 us -> none  [from_everyone(): lax.all_to_all(jnp.broadcast_to(value[None], (length, *value.shape)), axi...]
    unnamed x10 -> x7, local copies, waits for them, and re-layouts: 0.03 us -> 4.6 us
    all_to_all x1 -> x0, starting transfers between devices: 3.94 us -> none  [from_everyone(): lax.all_to_all(jnp.broadcast_to(value[None], (length, *value.shape)), axi...]
  transfers between devices with their start and end apart: 2 -> 0, of which waited for: 2 -> 0; matrix products, arithmetic and copies ran while one was open for 0% -> 0% of each run, Pallas kernels for 0% -> 0%
where the time goes in v1:
time: 252 us
  Pallas kernels  247 us (98%)
  local copies, waits for them, and re-layouts  4.6 us (2%)
    pallas_call x1, Pallas kernels, on_device(): pl.pallas_call(kernel, out_shape=(jax.ShapeDtypeStruct((mats, rows, width...  247 us

profile of v1, /device:TPU:1, one launch (start us, length us, event | category | flops | bytes accessed | tf_op | source)
XLA Modules:
  0.0 252.3 jit_solution(6751144182262289780)
XLA Ops:
  0.6 247.0 %shard_map.58 = (f32[2,512,640]{2,1,0:T(8,128)}, f32[2,512]{1,0:T(2,128)}, f32[2,640]{1,0:T(2,128)}) custom-call(bf16[1,2,512,10240]{3,2,1,0:T(8,128)(2,1)} %grad_hbm.1, f32[2,512]{1,0:T(2,128)} %row_moment.1, f32[2,640]{1,0:T(2,128)} %col_moment.1), custom_call_target="tpu_custom_call" | custom-call | tf_op jit(solution)/shard_map/pallas_call | solution.py:482
  247.7 0.0 copy-start.1
  247.7 0.0 copy-start
  247.7 3.4 %copy.9 = f32[2,512,640]{2,1,0:T(8,128)} copy(f32[2,512,640]{2,1,0:T(8,128)} %get-tuple-element.6) | data formatting | bytes 5242880
  251.1 0.0 copy-done.1
  251.1 0.6 copy.10
  251.7 0.0 copy-done
  251.7 0.6 copy.11
Async XLA Ops:
  247.7 3.4 %copy-start.1 = (f32[2,512]{1,0:T(2,128)S(1)}, f32[2,512]{1,0:T(2,128)}, u32[]{:S(2)}) copy-start(f32[2,512]{1,0:T(2,128)} %get-tuple-element.7) | copy-start | bytes 12292
  247.7 4.0 %copy-start = (f32[2,640]{1,0:T(2,128)S(1)}, f32[2,640]{1,0:T(2,128)}, u32[]{:S(2)}) copy-start(f32[2,640]{1,0:T(2,128)} %get-tuple-element.8) | copy-start | bytes 15364

commit v2 on v1

--- a/solution.py
+++ b/solution.py
@@ -13,25 +13,45 @@
 ROW = ("row_0", "row_1")
 RING = 4
 LANES = 128
-HALF = 8
+HALF = 16
 CHUNK = 2 * HALF
-X_SLOTS = 6
-X_AHEAD = 3
-S_SLOTS = 4
+X_SLOTS = 5
+X_AHEAD = 2
+S_SLOTS = 3
+TILE = 8
+LAGS = (1, 2, 3, 4)
 
 second_decay = 1.0 - 100.0 ** (-0.8)
 tiny_square = 1e-30
 
 
+def far_first(n_z, n_core):
+    def hops(step, n):
+        return min(step, n - step)
+
+    steps = [
+        (z, core, x, y)
+        for z in range(n_z)
+        for core in range(n_core)
+        for x in range(RING)
+        for y in range(RING)
+    ]
+    steps.sort(
+        key=lambda s: -(hops(s[0], n_z) + hops(s[2], RING) + hops(s[3], RING))
+    )
+    return [s for s in steps if any(s)]
+
+
 def wait_bytes(ref, sem):
     pltpu.make_async_copy(ref, ref, sem).wait()
 
 
 def kernel(
     grad_hbm,
-    row_moment,
-    col_moment,
+    row_hbm,
+    col_hbm,
     update,
+    factor,
     new_rows,
     new_cols,
     x_in,
@@ -40,15 +60,18 @@
     sum1,
     land2,
     sum2,
-    grad,
+    row_moment,
+    col_moment,
     row_part,
     col_part,
+    weighted,
+    weighted_row,
     row_scale,
     row_land,
     col_land,
     all_land,
-    fin_land,
     x_sem,
+    m_sem,
     send0,
     send1,
     send2,
@@ -61,6 +84,7 @@
     stat_recv,
 ):
     mats, rows = row_moment.shape
+    offsets = far_first(lax.axis_size("row_0"), lax.axis_size("row_1"))
     width = col_moment.shape[1]
     block = RING * width
     row_groups = rows // LANES
@@ -77,6 +101,8 @@
 
     def at(axis, step):
         return lax.rem(here[axis] + (step + RING), RING)
+
+    me = my_row * n_col + my_col
 
     def neighbour(axis, step):
         return {COL[axis]: at(axis, step)}
@@ -272,10 +298,11 @@
                 here_rows = pl.ds(
                     pl.multiple_of(r + color * CHUNK + half * HALF, HALF), HALF
                 )
-                grad[m, here_rows, :] = g
+                update[m, here_rows, :] = g
                 squares = g * g + tiny_square
                 row_part[m, here_rows, :] = lane_tiles(squares)
-                squares_sum = squares_sum + squares
+                for t in range(HALF // TILE):
+                    squares_sum = squares_sum + squares[t * TILE : (t + 1) * TILE]
         col_part[m] = squares_sum
 
     def pick(ref, m, lanes):
@@ -288,57 +315,39 @@
             def _():
                 ref[i : i + 1, lanes] = value
 
-    def all_cols(m, buf, which):
-        mine = buf.at[m, my_col]
-
-        def one(d, _):
-            send(mine, mine, stat_send.at[m, which], stat_recv.at[m, which], col_peer(d))
+    def lane_major(part):
+        return jnp.sum(part.T, axis=0, keepdims=True)
+
+    def group(b):
+        return slice(b * LANES, (b + 1) * LANES)
+
+    def share_sums(m):
+        for b in range(row_groups):
+            row_land[m, my_col, b : b + 1, :] = lane_major(row_part[m, group(b), :])
+        col_land[m, my_row] = jnp.sum(col_part[m], axis=0, keepdims=True)
+        mine = col_land.at[m, my_row]
+
+        def to_row(d, _):
+            send(mine, mine, stat_send.at[m, 0], stat_recv.at[m, 0], row_peer(d))
             return 0
 
-        lax.fori_loop(1, n_col, one, 0)
-
-    def all_rows(m, buf, which):
-        mine = buf.at[m, my_row]
-
-        def one(d, _):
-            send(mine, mine, stat_send.at[m, which], stat_recv.at[m, which], row_peer(d))
+        lax.fori_loop(1, n_row, to_row, 0)
+        rows_mine = row_land.at[m, my_col]
+
+        def to_col(d, _):
+            send(
+                rows_mine, rows_mine, stat_send.at[m, 1], stat_recv.at[m, 1], col_peer(d)
+            )
             return 0
 
-        lax.fori_loop(1, n_row, one, 0)
-
-    def wait_all(m, buf, which, n):
+        lax.fori_loop(1, n_col, to_col, 0)
+
+    def all_but_one(m, buf, sem, n):
         if n > 1:
-            wait_bytes(buf.at[m, pl.ds(0, n - 1)], stat_recv.at[m, which])
-
-    def wait_sent(m, buf, which, n):
-        if n > 1:
-            wait_bytes(buf.at[m, pl.ds(0, n - 1)], stat_send.at[m, which])
-
-    def statistics1(m):
-        for b in range(row_groups):
-            part = row_part[m, b * LANES : (b + 1) * LANES, :]
-            row_land[m, my_col, b : b + 1, :] = jnp.sum(part.T, axis=0, keepdims=True)
-        col_land[m, my_row] = jnp.sum(col_part[m], axis=0, keepdims=True)
-        all_cols(m, row_land, 0)
-        all_rows(m, col_land, 1)
-
-    def statistics2(m):
-        wait_all(m, row_land, 0, n_col)
-        wait_all(m, col_land, 1, n_row)
-        full = row_land[m, 0]
-        for s in range(1, n_col):
-            full = full + row_land[m, s]
-        moments = []
-        for b in range(row_groups):
-            moment = (
-                second_decay * pick(row_moment, m, slice(b * LANES, (b + 1) * LANES))
-                + (1.0 - second_decay) * full[b : b + 1] / total_cols
-            )
-            put(new_rows, m, slice(b * LANES, (b + 1) * LANES), moment)
-            moments.append(moment)
-            row_scale[b * LANES : (b + 1) * LANES, :] = jnp.broadcast_to(
-                lax.rsqrt(moment), (LANES, LANES)
-            ).T
+            wait_bytes(buf.at[m, pl.ds(0, n - 1)], sem)
+
+    def share_clip(m):
+        all_but_one(m, col_land, stat_recv.at[m, 0], n_row)
         full = col_land[m, 0]
         for s in range(1, n_row):
             full = full + col_land[m, s]
@@ -347,68 +356,78 @@
             + (1.0 - second_decay) * full / total_rows
         )
         put(new_cols, m, slice(None), col)
-        col_scale = jnp.broadcast_to(lax.rsqrt(col), (HALF, width))
-
-        def rescale(t, total):
-            r = pl.ds(pl.multiple_of(t * HALF, HALF), HALF)
+        inverse = jnp.broadcast_to(1.0 / col, (TILE, width))
+
+        def weigh(t, _):
+            r = pl.ds(pl.multiple_of(t * TILE, TILE), TILE)
+            v = update[m, r, :]
+            weighted[r, :] = lane_tiles(v * v * inverse)
+            return 0
+
+        lax.fori_loop(0, rows // TILE, weigh, 0)
+        for b in range(row_groups):
+            weighted_row[b : b + 1, :] = lane_major(weighted[group(b), :])
+
+        all_but_one(m, row_land, stat_recv.at[m, 1], n_col)
+        full = row_land[m, 0]
+        for s in range(1, n_col):
+            full = full + row_land[m, s]
+        moments, clip, level = [], None, None
+        for b in range(row_groups):
+            moment = (
+                second_decay * pick(row_moment, m, group(b))
+                + (1.0 - second_decay) * full[b : b + 1] / total_cols
+            )
+            part = weighted_row[b : b + 1, :] / moment
+            clip = part if clip is None else clip + part
+            level = moment if level is None else level + moment
+            moments.append(moment)
+        all_land[m, me, 0:1, :] = clip
+        all_land[m, me, 1:2, :] = level
+        mine = all_land.at[m, me]
+        for step in offsets:
+            z, core, x, y = step
+            there = {
+                "row_0": lax.rem(lax.axis_index("row_0") + z, n_row0),
+                "row_1": lax.rem(lax.axis_index("row_1") + core, n_row1),
+                "col_0": at(0, x),
+                "col_1": at(1, y),
+            }
+            send(mine, mine, stat_send.at[m, 2], stat_recv.at[m, 2], there)
+        for b in range(row_groups):
+            put(new_rows, m, group(b), moments[b])
+            row_scale[group(b), :] = jnp.broadcast_to(
+                lax.rsqrt(moments[b]), (LANES, LANES)
+            ).T
+        col_scale = jnp.broadcast_to(lax.rsqrt(col), (TILE, width))
+
+        def rescale(t, _):
+            r = pl.ds(pl.multiple_of(t * TILE, TILE), TILE)
             scale = row_scale[r, :]
             for c in range(width // LANES):
-                lanes = slice(c * LANES, (c + 1) * LANES)
-                v = grad[m, r, lanes] * col_scale[:, lanes] * scale
-                update[m, r, lanes] = v
-                total = total + v * v
-            return total
-
-        total = lax.fori_loop(
-            0, rows // HALF, rescale, jnp.zeros((HALF, LANES), jnp.float32)
-        )
-        level = moments[0]
-        for moment in moments[1:]:
-            level = level + moment
-        all_land[m, my_col] = total
-        fin_land[m, my_row, HALF : HALF + 1, :] = level
-        all_cols(m, all_land, 2)
-
-    def statistics3(m):
-        wait_all(m, all_land, 2, n_col)
-        total = all_land[m, 0]
-        for s in range(1, n_col):
-            total = total + all_land[m, s]
-        fin_land[m, my_row, :HALF, :] = total
-        all_rows(m, fin_land, 3)
-
-    def statistics4(m):
-        wait_all(m, fin_land, 3, n_row)
-        total = fin_land[m, 0]
-        for s in range(1, n_row):
-            total = total + fin_land[m, s]
-        level = jnp.sum(total[HALF : HALF + 1], axis=1, keepdims=True) / total_rows
-        clip = jnp.sum(
-            jnp.sum(total[:HALF], axis=0, keepdims=True), axis=1, keepdims=True
-        )
+                lanes = group(c)
+                update[m, r, lanes] = update[m, r, lanes] * col_scale[:, lanes] * scale
+            return 0
+
+        lax.fori_loop(0, rows // TILE, rescale, 0)
+
+    def finish(m):
+        all_but_one(m, all_land, stat_recv.at[m, 2], n_row * n_col)
+        total = jnp.sum(all_land[m], axis=0)
+        level = jnp.sum(total[1:2], axis=1, keepdims=True) / (n_col * total_rows)
+        clip = jnp.sum(total[0:1], axis=1, keepdims=True)
         clip_scale = jnp.maximum(
             1.0, jnp.sqrt(clip * level / (total_rows * total_cols))
         )
-        factor = jnp.broadcast_to(jnp.sqrt(level) / clip_scale, (HALF, width))
-
-        def finish(t, _):
-            r = pl.ds(pl.multiple_of(t * HALF, HALF), HALF)
-            update[m, r, :] = update[m, r, :] * factor
-            return 0
-
-        lax.fori_loop(0, rows // HALF, finish, 0)
-        wait_sent(m, row_land, 0, n_col)
-        wait_sent(m, col_land, 1, n_row)
-        wait_sent(m, all_land, 2, n_col)
-        wait_sent(m, fin_land, 3, n_row)
+        scale = jnp.broadcast_to(jnp.sqrt(level) / clip_scale, (TILE, LANES))
+        factor[m] = scale
+        all_but_one(m, col_land, stat_send.at[m, 0], n_row)
+        all_but_one(m, row_land, stat_send.at[m, 1], n_col)
+        all_but_one(m, all_land, stat_send.at[m, 2], n_row * n_col)
 
     barrier = pltpu.get_barrier_semaphore()
-
-    def greet_col(d, _):
-        pl.semaphore_signal(
-            barrier, inc=1, device_id=col_peer(d), device_id_type=MESH
-        )
-        return 0
+    row_copy = pltpu.make_async_copy(row_hbm, row_moment, m_sem.at[0])
+    col_copy = pltpu.make_async_copy(col_hbm, col_moment, m_sem.at[1])
 
     def greet_row(d, _):
         pl.semaphore_signal(
@@ -418,12 +437,19 @@
 
     for k in range(X_AHEAD):
         load(k).start()
-    lax.fori_loop(1, n_col, greet_col, 0)
+    for axis in range(2):
+        for to in (1, -1):
+            pl.semaphore_signal(
+                barrier, inc=1, device_id=neighbour(axis, to), device_id_type=MESH
+            )
     lax.fori_loop(1, n_row, greet_row, 0)
     col_part[...] = jnp.zeros_like(col_part)
-    fin_land[...] = jnp.zeros_like(fin_land)
+    row_copy.start()
+    col_copy.start()
     prepare(0)
-    pl.semaphore_wait(barrier, n_col - 1 + n_row - 1)
+    pl.semaphore_wait(barrier, 4 + n_row - 1)
+    row_copy.wait()
+    col_copy.wait()
 
     def step(it, _):
         @pl.when(it < chunks)
@@ -434,7 +460,7 @@
             def _():
                 load(it + X_AHEAD).start()
 
-        for lag, work in ((1, stage1), (2, stage2), (3, stage3), (4, stage4)):
+        for lag, work in zip(LAGS, (stage1, stage2, stage3, stage4)):
 
             @pl.when((it >= lag) & (it < chunks + lag))
             def _():
@@ -445,10 +471,9 @@
             prepare(it + 1)
 
         for when, work in (
-            ((per_mat + 3, chunks + 3), statistics1),
-            ((per_mat + 5, chunks + 4), statistics2),
-            ((per_mat + 7, chunks + 5), statistics3),
-            ((per_mat + 9, chunks + 6), statistics4),
+            ((per_mat - 1 + LAGS[3], chunks - 1 + LAGS[3]), share_sums),
+            ((per_mat + 1 + LAGS[3], chunks + LAGS[3]), share_clip),
+            ((per_mat + 3 + LAGS[3], chunks + 1 + LAGS[3]), finish),
         ):
 
             @pl.when((it == when[0]) | (it == when[1]))
@@ -457,7 +482,7 @@
 
         return 0
 
-    lax.fori_loop(0, chunks + 7, step, 0)
+    lax.fori_loop(0, chunks + 2 + LAGS[3], step, 0)
 
     def drain(slot, _):
         for color in range(2):
@@ -468,6 +493,38 @@
         return 0
 
     lax.fori_loop(0, S_SLOTS, drain, 0)
+
+
+def finish_kernel(
+    scaled, factor, new_rows, new_cols, update_hbm, rows_hbm, cols_hbm, out, sems
+):
+    mats, rows, width = scaled.shape
+    pieces = 4
+    copies = [
+        pltpu.make_async_copy(new_rows, rows_hbm, sems.at[0]),
+        pltpu.make_async_copy(new_cols, cols_hbm, sems.at[1]),
+    ]
+    for copy in copies:
+        copy.start()
+    size = rows // pieces
+    for m in range(mats):
+        scale = jnp.broadcast_to(factor[m][:, :1], (TILE, width))
+        for p in range(pieces):
+
+            def one(t, _):
+                r = pl.ds(pl.multiple_of(p * size + t * TILE, TILE), TILE)
+                out[m, r, :] = scaled[m, r, :] * scale
+                return 0
+
+            lax.fori_loop(0, size // TILE, one, 0, unroll=True)
+            here = pl.ds(p * size, size)
+            copy = pltpu.make_async_copy(
+                out.at[m, here], update_hbm.at[m, here], sems.at[2 + m * pieces + p]
+            )
+            copy.start()
+            copies.append(copy)
+    for copy in copies:
+        copy.wait()
 
 
 def on_device(grad_terms, row_moment, col_moment):
@@ -478,16 +535,19 @@
     chunks = mats * rows // (2 * CHUNK)
     f32 = jnp.float32
     vmem = pl.BlockSpec(memory_space=pltpu.VMEM)
+    hbm = pl.BlockSpec(memory_space=pltpu.HBM)
     dma = pltpu.SemaphoreType.DMA
-    return pl.pallas_call(
+    shapes = (
+        jax.ShapeDtypeStruct((mats, rows, width), f32),
+        jax.ShapeDtypeStruct((mats, TILE, LANES), f32),
+        jax.ShapeDtypeStruct((mats, rows), f32),
+        jax.ShapeDtypeStruct((mats, width), f32),
+    )
+    scaled, factor, new_rows, new_cols = pl.pallas_call(
         kernel,
-        out_shape=(
-            jax.ShapeDtypeStruct((mats, rows, width), f32),
-            jax.ShapeDtypeStruct((mats, rows), f32),
-            jax.ShapeDtypeStruct((mats, width), f32),
-        ),
-        in_specs=[pl.BlockSpec(memory_space=pl.ANY), vmem, vmem],
-        out_specs=(vmem, vmem, vmem),
+        out_shape=shapes,
+        in_specs=[hbm, hbm, hbm],
+        out_specs=(vmem, vmem, vmem, vmem),
         scratch_shapes=[
             pltpu.VMEM((X_SLOTS, 2 * CHUNK, n_col * width), jnp.bfloat16),
             pltpu.VMEM((S_SLOTS, 2, 4, HALF, RING * width), f32),
@@ -495,15 +555,18 @@
             pltpu.VMEM((chunks, 2, 4, HALF, RING * width), f32),
             pltpu.VMEM((chunks, 2, 2, HALF, width), f32),
             pltpu.VMEM((chunks, 2, 4, HALF, width), f32),
-            pltpu.VMEM((mats, rows, width), f32),
+            pltpu.VMEM((mats, rows), f32),
+            pltpu.VMEM((mats, width), f32),
             pltpu.VMEM((mats, rows, LANES), f32),
-            pltpu.VMEM((mats, HALF, width), f32),
+            pltpu.VMEM((mats, TILE, width), f32),
+            pltpu.VMEM((rows, LANES), f32),
+            pltpu.VMEM((rows // LANES, LANES), f32),
             pltpu.VMEM((rows, LANES), f32),
             pltpu.VMEM((mats, n_col, rows // LANES, LANES), f32),
             pltpu.VMEM((mats, n_row, 1, width), f32),
-            pltpu.VMEM((mats, n_col, HALF, LANES), f32),
-            pltpu.VMEM((mats, n_row, 2 * HALF, LANES), f32),
+            pltpu.VMEM((mats, n_row * n_col, 2, LANES), f32),
             dma((X_SLOTS,)),
+            dma((2,)),
             dma((S_SLOTS, 2)),
             dma((S_SLOTS, 2)),
             dma((S_SLOTS, 2)),
@@ -512,15 +575,23 @@
             dma((chunks, 2)),
             dma((chunks, 2)),
             dma((chunks, 2)),
-            dma((mats, 4)),
-            dma((mats, 4)),
+            dma((mats, 3)),
+            dma((mats, 3)),
         ],
         compiler_params=pltpu.CompilerParams(
             collective_id=0,
             has_side_effects=True,
-            vmem_limit_bytes=60 * 1024 * 1024,
+            vmem_limit_bytes=50 * 1024 * 1024,
         ),
     )(grad_terms, row_moment, col_moment)
+    return pl.pallas_call(
+        finish_kernel,
+        out_shape=(shapes[0], shapes[2], shapes[3]),
+        in_specs=[vmem] * 4,
+        out_specs=(hbm, hbm, hbm),
+        scratch_shapes=[pltpu.VMEM((mats, rows, width), f32), dma((10,))],
+        compiler_params=pltpu.CompilerParams(vmem_limit_bytes=4 * 1024 * 1024),
+    )(scaled, factor, new_rows, new_cols)
 
 
 def solution(mesh):

time: 252 us -> 241 us (0.956)
  Pallas kernels: 247 us -> 239 us
  local copies, waits for them, and re-layouts: 4.6 us -> 1.37 us
    pallas_call x1 -> x2, Pallas kernels: 247 us -> 239 us  [the longest x1 237 us: on_device(): pl.pallas_call(kernel, out_shape=shapes, in_specs=[hbm, hbm, hbm], out_sp...]
    unnamed x7 -> x4, local copies, waits for them, and re-layouts: 4.6 us -> 1.37 us
where the time goes in v2:
time: 241 us
  Pallas kernels  239 us (99%)
    pallas_call x1, Pallas kernels, on_device(): pl.pallas_call(kernel, out_shape=shapes, in_specs=[hbm, hbm, hbm], out_sp...  237 us

profile of v2, /device:TPU:1, one launch (start us, length us, event | category | flops | bytes accessed | tf_op | source)
XLA Modules:
  0.0 240.7 jit_solution(7647789435884920034)
XLA Ops:
  0.6 0.0 copy-start
  0.6 0.7 copy-done
  1.3 0.0 copy-start.1
  1.3 0.7 copy-done.1
  2.0 237.0 %shard_map.58 = (f32[2,512,640]{2,1,0:T(8,128)S(1)}, f32[2,8,128]{2,1,0:T(8,128)S(1)}, f32[2,512]{1,0:T(2,128)S(1)}, f32[2,640]{1,0:T(2,128)S(1)}) custom-call(bf16[1,2,512,10240]{3,2,1,0:T(8,128)(2,1)} %grad_hbm.1, f32[2,512]{1,0:T(2,128)S(1)} %copy-done.1, f32[2,640]{1,0:T(2,128)S(1)} %copy-done), custom_call_target="tpu_custom_call" | custom-call | tf_op jit(solution)/shard_map/pallas_call | solution.py:546
  239.0 1.7 shard_map.59
Async XLA Ops:
  0.6 0.7 copy-start
  1.3 0.7 copy-start.1

commit v3 on v2

--- a/solution.py
+++ b/solution.py
@@ -19,7 +19,7 @@
 X_AHEAD = 2
 S_SLOTS = 3
 TILE = 8
-LAGS = (1, 2, 3, 4)
+R_SLOTS = 6
 
 second_decay = 1.0 - 100.0 ** (-0.8)
 tiny_square = 1e-30
@@ -76,6 +76,7 @@
     send1,
     send2,
     send3,
+    send5,
     recv1,
     recv2,
     recv3,
@@ -125,21 +126,24 @@
             device_id_type=MESH,
         ).start()
 
-    def load(k):
+    def load(k, color):
         slot = lax.rem(k, X_SLOTS)
         m = k // per_mat
-        r = pl.multiple_of(lax.rem(k, per_mat) * (2 * CHUNK), 2 * CHUNK)
+        r = lax.rem(k, per_mat) * (2 * CHUNK) + color * CHUNK
         return pltpu.make_async_copy(
-            grad_hbm.at[0, m, pl.ds(r, 2 * CHUNK), :], x_in.at[slot], x_sem.at[slot]
+            grad_hbm.at[0, m, pl.ds(pl.multiple_of(r, CHUNK), CHUNK), :],
+            x_in.at[slot, color],
+            x_sem.at[slot, color],
         )
+
+    def start_load(k):
+        for color in range(2):
+            load(k, color).start()
 
     def own(color, k, idx, seg):
         outer, inner = (idx, seg) if color == 0 else (seg, idx)
         c = pl.multiple_of(outer * block + inner * width, LANES)
-        v = x_in[
-            lax.rem(k, X_SLOTS), color * CHUNK : (color + 1) * CHUNK, pl.ds(c, width)
-        ]
-        v = v.astype(jnp.float32)
+        v = x_in[lax.rem(k, X_SLOTS), color, :, pl.ds(c, width)].astype(jnp.float32)
         return v[:HALF], v[HALF:]
 
     def cols(s):
@@ -148,52 +152,68 @@
     def inner_cols(idx):
         return pl.ds(pl.multiple_of(idx * width, LANES), width)
 
+    def free_stage(k, color):
+        slot = lax.rem(k, S_SLOTS)
+
+        @pl.when(k >= S_SLOTS)
+        def _():
+            wait_bytes(stage.at[slot, color], send0.at[slot, color])
+
+    def prepare_relay(k, color):
+        slot = lax.rem(k, S_SLOTS)
+        for s in range(RING):
+            top, low = own(color, k, at(color, 2), s)
+            stage[slot, color, 0, :, cols(s)] = top
+            stage[slot, color, 1, :, cols(s)] = low
+
+    def prepare_direct(k, color):
+        slot = lax.rem(k, S_SLOTS)
+        for s in range(RING):
+            _, low = own(color, k, at(color, 1), s)
+            stage[slot, color, 2, :, cols(s)] = low
+            top, _ = own(color, k, at(color, -1), s)
+            stage[slot, color, 3, :, cols(s)] = top
+
     def prepare(k):
+        for color in range(2):
+            load(k, color).wait()
+            free_stage(k, color)
+            prepare_relay(k, color)
+            prepare_direct(k, color)
+
+    def send_relay(k, color):
         slot = lax.rem(k, S_SLOTS)
-        load(k).wait()
-        for color in range(2):
-
-            @pl.when(k >= S_SLOTS)
-            def _():
-                wait_bytes(stage.at[slot, color], send0.at[slot, color])
-
-            axis = color
-            for s in range(RING):
-                top, low = own(color, k, at(axis, 2), s)
-                stage[slot, color, 0, :, cols(s)] = top
-                stage[slot, color, 1, :, cols(s)] = low
-            for s in range(RING):
-                _, low = own(color, k, at(axis, 1), s)
-                stage[slot, color, 2, :, cols(s)] = low
-                top, _ = own(color, k, at(axis, -1), s)
-                stage[slot, color, 3, :, cols(s)] = top
+        for which, step in ((0, 1), (1, -1)):
+            send(
+                stage.at[slot, color, which],
+                land1.at[k, color, which],
+                send0.at[slot, color],
+                recv1.at[lax.rem(k, R_SLOTS), color],
+                neighbour(color, step),
+            )
+
+    def send_direct(k, color):
+        slot = lax.rem(k, S_SLOTS)
+        for which, step in ((2, 1), (3, -1)):
+            send(
+                stage.at[slot, color, which],
+                sum1.at[k, color, which],
+                send0.at[slot, color],
+                recv2.at[lax.rem(k, R_SLOTS), color],
+                neighbour(color, step),
+            )
 
     def stage0(k):
-        slot = lax.rem(k, S_SLOTS)
-        for which, step, land in ((0, 1, 0), (1, -1, 1)):
-            for color in range(2):
-                send(
-                    stage.at[slot, color, which],
-                    land1.at[k, color, land],
-                    send0.at[slot, color],
-                    recv1.at[k, color],
-                    neighbour(color, step),
-                )
-        for which, step in ((2, 1), (3, -1)):
-            for color in range(2):
-                send(
-                    stage.at[slot, color, which],
-                    sum1.at[k, color, which],
-                    send0.at[slot, color],
-                    recv2.at[k, color],
-                    neighbour(color, step),
-                )
+        for color in range(2):
+            send_relay(k, color)
+        for color in range(2):
+            send_direct(k, color)
 
     def stage1(k):
         slot = lax.rem(k, S_SLOTS)
         for color in range(2):
             axis = color
-            wait_bytes(land1.at[k, color], recv1.at[k, color])
+            wait_bytes(land1.at[k, color], recv1.at[lax.rem(k, R_SLOTS), color])
 
             @pl.when(k >= S_SLOTS)
             def _():
@@ -209,7 +229,7 @@
                     land1.at[k, color, which],
                     sum1.at[k, color, which],
                     send1.at[slot, color],
-                    recv2.at[k, color],
+                    recv2.at[lax.rem(k, R_SLOTS), color],
                     neighbour(axis, step),
                 )
 
@@ -217,11 +237,11 @@
         slot = lax.rem(k, S_SLOTS)
         for color in range(2):
             axis = color
-            wait_bytes(sum1.at[k, color], recv2.at[k, color])
+            wait_bytes(sum1.at[k, color], recv2.at[lax.rem(k, R_SLOTS), color])
 
             @pl.when(k >= S_SLOTS)
             def _():
-                wait_bytes(sum2.at[k, color], send2.at[slot, color])
+                wait_bytes(land2.at[k, color], send2.at[slot, color])
 
             for s in range(RING):
                 top, low = own(color, k, at(axis, 0), s)
@@ -241,14 +261,24 @@
                     sum1.at[k, color, which, :, inner_cols(at(axis, 2))],
                     land2.at[k, color, which],
                     send2.at[slot, color],
-                    recv3.at[k, color],
+                    recv3.at[lax.rem(k, R_SLOTS), color],
                     neighbour(axis, step),
                 )
+
+    def stage2_direct(k):
+        slot = lax.rem(k, per_mat)
+        for color in range(2):
+            axis = 1 - color
+
+            @pl.when(k >= per_mat)
+            def _():
+                wait_bytes(land2.at[k, color], send5.at[slot, color])
+
             for half, which, step in ((1, 2, 1), (0, 3, -1)):
                 send(
                     sum1.at[k, color, half, :, inner_cols(at(axis, step))],
                     sum2.at[k, color, which],
-                    send2.at[slot, color],
+                    send5.at[slot, color],
                     recv4.at[k, color],
                     neighbour(axis, step),
                 )
@@ -257,7 +287,7 @@
         slot = lax.rem(k, S_SLOTS)
         for color in range(2):
             axis = 1 - color
-            wait_bytes(land2.at[k, color], recv3.at[k, color])
+            wait_bytes(land2.at[k, color], recv3.at[lax.rem(k, R_SLOTS), color])
 
             @pl.when(k >= S_SLOTS)
             def _():
@@ -321,26 +351,39 @@
     def group(b):
         return slice(b * LANES, (b + 1) * LANES)
 
+    def early_sums(m):
+        for b in range(row_groups - 1):
+            row_land[m, my_col, b : b + 1, :] = lane_major(row_part[m, group(b), :])
+
+    def peer(step):
+        z, core, x, y = step
+        there = {}
+        if z or core:
+            there["row_0"] = lax.rem(lax.axis_index("row_0") + z, n_row0)
+            there["row_1"] = lax.rem(lax.axis_index("row_1") + core, n_row1)
+        if x or y:
+            there["col_0"] = at(0, x)
+            there["col_1"] = at(1, y)
+        return there
+
     def share_sums(m):
-        for b in range(row_groups):
-            row_land[m, my_col, b : b + 1, :] = lane_major(row_part[m, group(b), :])
         col_land[m, my_row] = jnp.sum(col_part[m], axis=0, keepdims=True)
         mine = col_land.at[m, my_row]
-
-        def to_row(d, _):
-            send(mine, mine, stat_send.at[m, 0], stat_recv.at[m, 0], row_peer(d))
-            return 0
-
-        lax.fori_loop(1, n_row, to_row, 0)
+        for step in offsets:
+            if not any(step[2:]):
+                send(mine, mine, stat_send.at[m, 0], stat_recv.at[m, 0], peer(step))
+        b = row_groups - 1
+        row_land[m, my_col, b : b + 1, :] = lane_major(row_part[m, group(b), :])
         rows_mine = row_land.at[m, my_col]
-
-        def to_col(d, _):
-            send(
-                rows_mine, rows_mine, stat_send.at[m, 1], stat_recv.at[m, 1], col_peer(d)
-            )
-            return 0
-
-        lax.fori_loop(1, n_col, to_col, 0)
+        for step in offsets:
+            if not any(step[:2]):
+                send(
+                    rows_mine,
+                    rows_mine,
+                    stat_send.at[m, 1],
+                    stat_recv.at[m, 1],
+                    peer(step),
+                )
 
     def all_but_one(m, buf, sem, n):
         if n > 1:
@@ -355,7 +398,6 @@
             second_decay * pick(col_moment, m, slice(None))
             + (1.0 - second_decay) * full / total_rows
         )
-        put(new_cols, m, slice(None), col)
         inverse = jnp.broadcast_to(1.0 / col, (TILE, width))
 
         def weigh(t, _):
@@ -364,7 +406,7 @@
             weighted[r, :] = lane_tiles(v * v * inverse)
             return 0
 
-        lax.fori_loop(0, rows // TILE, weigh, 0)
+        lax.fori_loop(0, rows // TILE, weigh, 0, unroll=8)
         for b in range(row_groups):
             weighted_row[b : b + 1, :] = lane_major(weighted[group(b), :])
 
@@ -386,14 +428,8 @@
         all_land[m, me, 1:2, :] = level
         mine = all_land.at[m, me]
         for step in offsets:
-            z, core, x, y = step
-            there = {
-                "row_0": lax.rem(lax.axis_index("row_0") + z, n_row0),
-                "row_1": lax.rem(lax.axis_index("row_1") + core, n_row1),
-                "col_0": at(0, x),
-                "col_1": at(1, y),
-            }
-            send(mine, mine, stat_send.at[m, 2], stat_recv.at[m, 2], there)
+            send(mine, mine, stat_send.at[m, 2], stat_recv.at[m, 2], peer(step))
+        put(new_cols, m, slice(None), col)
         for b in range(row_groups):
             put(new_rows, m, group(b), moments[b])
             row_scale[group(b), :] = jnp.broadcast_to(
@@ -409,11 +445,14 @@
                 update[m, r, lanes] = update[m, r, lanes] * col_scale[:, lanes] * scale
             return 0
 
-        lax.fori_loop(0, rows // TILE, rescale, 0)
+        lax.fori_loop(0, rows // TILE, rescale, 0, unroll=8)
 
     def finish(m):
         all_but_one(m, all_land, stat_recv.at[m, 2], n_row * n_col)
-        total = jnp.sum(all_land[m], axis=0)
+        parts = [all_land[m, s] for s in range(4)]
+        for s in range(4, n_row * n_col):
+            parts[s % 4] = parts[s % 4] + all_land[m, s]
+        total = (parts[0] + parts[1]) + (parts[2] + parts[3])
         level = jnp.sum(total[1:2], axis=1, keepdims=True) / (n_col * total_rows)
         clip = jnp.sum(total[0:1], axis=1, keepdims=True)
         clip_scale = jnp.maximum(
@@ -421,6 +460,18 @@
         )
         scale = jnp.broadcast_to(jnp.sqrt(level) / clip_scale, (TILE, LANES))
         factor[m] = scale
+
+        @pl.when(m < mats - 1)
+        def _():
+            wide = jnp.broadcast_to(scale[:, :1], (TILE, width))
+
+            def one(t, _):
+                r = pl.ds(pl.multiple_of(t * TILE, TILE), TILE)
+                update[m, r, :] = update[m, r, :] * wide
+                return 0
+
+            lax.fori_loop(0, rows // TILE, one, 0, unroll=4)
+
         all_but_one(m, col_land, stat_send.at[m, 0], n_row)
         all_but_one(m, row_land, stat_send.at[m, 1], n_col)
         all_but_one(m, all_land, stat_send.at[m, 2], n_row * n_col)
@@ -435,8 +486,7 @@
         )
         return 0
 
-    for k in range(X_AHEAD):
-        load(k).start()
+    start_load(0)
     for axis in range(2):
         for to in (1, -1):
             pl.semaphore_signal(
@@ -446,23 +496,39 @@
     col_part[...] = jnp.zeros_like(col_part)
     row_copy.start()
     col_copy.start()
-    prepare(0)
+    load(0, 0).wait()
+    prepare_relay(0, 0)
     pl.semaphore_wait(barrier, 4 + n_row - 1)
+    send_relay(0, 0)
+    load(0, 1).wait()
+    prepare_relay(0, 1)
+    send_relay(0, 1)
+    for k in range(1, 1 + X_AHEAD):
+        start_load(k)
+    for color in range(2):
+        prepare_direct(0, color)
+        send_direct(0, color)
     row_copy.wait()
     col_copy.wait()
 
     def step(it, _):
-        @pl.when(it < chunks)
+        @pl.when(it > 0)
         def _():
             stage0(it)
 
             @pl.when(it + X_AHEAD < chunks)
             def _():
-                load(it + X_AHEAD).start()
-
-        for lag, work in zip(LAGS, (stage1, stage2, stage3, stage4)):
-
-            @pl.when((it >= lag) & (it < chunks + lag))
+                start_load(it + X_AHEAD)
+
+        for lag, work, end in (
+            (3, stage2_direct, per_mat),
+            (1, stage1, chunks),
+            (2, stage2, chunks),
+            (3, stage3, chunks),
+            (4, stage4, per_mat),
+        ):
+
+            @pl.when((it >= lag) & (it < end + lag))
             def _():
                 work(it - lag)
 
@@ -471,28 +537,67 @@
             prepare(it + 1)
 
         for when, work in (
-            ((per_mat - 1 + LAGS[3], chunks - 1 + LAGS[3]), share_sums),
-            ((per_mat + 1 + LAGS[3], chunks + LAGS[3]), share_clip),
-            ((per_mat + 3 + LAGS[3], chunks + 1 + LAGS[3]), finish),
+            (per_mat + 3, early_sums),
+            (per_mat + 3, share_sums),
+            (per_mat + 5, share_clip),
+            (per_mat + 7, finish),
         ):
 
-            @pl.when((it == when[0]) | (it == when[1]))
+            @pl.when(it == when)
             def _():
-                work(jnp.where(it == when[0], 0, 1))
+                work(0)
 
         return 0
 
-    lax.fori_loop(0, chunks + 2 + LAGS[3], step, 0)
+    lax.fori_loop(0, chunks, step, 0)
+
+    def direct(first, count):
+        def one(k, _):
+            stage2_direct(k)
+            return 0
+
+        lax.fori_loop(first, first + count, one, 0)
+
+    last = chunks - 1
+    share = per_mat // 4
+    stage1(last)
+    direct(per_mat, share)
+    stage2(last - 1)
+    stage3(last - 2)
+    direct(per_mat + share, share)
+    stage2(last)
+    direct(per_mat + 2 * share, share)
+    stage3(last - 1)
+    direct(per_mat + 3 * share, per_mat - 3 * share)
+    stage3(last)
+
+    def finish_chunk(k, _):
+        stage4(k)
+        return 0
+
+    lax.fori_loop(per_mat, last, finish_chunk, 0)
+    early_sums(mats - 1)
+    stage4(last)
+    share_sums(mats - 1)
+    share_clip(mats - 1)
+    finish(mats - 1)
 
     def drain(slot, _):
         for color in range(2):
             wait_bytes(stage.at[slot, color], send0.at[slot, color])
             wait_bytes(land1.at[0, color], send1.at[slot, color])
-            wait_bytes(sum2.at[0, color], send2.at[slot, color])
+            wait_bytes(land2.at[0, color], send2.at[slot, color])
             wait_bytes(land2.at[0, color], send3.at[slot, color])
         return 0
 
     lax.fori_loop(0, S_SLOTS, drain, 0)
+
+    def drain_direct(slot, _):
+        for color in range(2):
+            wait_bytes(land2.at[0, color], send5.at[slot, color])
+        return 0
+
+    lax.fori_loop(0, per_mat, drain_direct, 0)
 
 
 def finish_kernel(
@@ -500,29 +605,26 @@
 ):
     mats, rows, width = scaled.shape
     pieces = 4
-    copies = [
-        pltpu.make_async_copy(new_rows, rows_hbm, sems.at[0]),
-        pltpu.make_async_copy(new_cols, cols_hbm, sems.at[1]),
-    ]
-    for copy in copies:
+    last = mats - 1
+    size = rows // pieces
+    copies = []
+
+    def start(src, dst):
+        copy = pltpu.make_async_copy(src, dst, sems.at[len(copies)])
         copy.start()
-    size = rows // pieces
-    for m in range(mats):
-        scale = jnp.broadcast_to(factor[m][:, :1], (TILE, width))
-        for p in range(pieces):
-
-            def one(t, _):
-                r = pl.ds(pl.multiple_of(p * size + t * TILE, TILE), TILE)
-                out[m, r, :] = scaled[m, r, :] * scale
-                return 0
-
-            lax.fori_loop(0, size // TILE, one, 0, unroll=True)
-            here = pl.ds(p * size, size)
-            copy = pltpu.make_async_copy(
-                out.at[m, here], update_hbm.at[m, here], sems.at[2 + m * pieces + p]
-            )
-            copy.start()
-            copies.append(copy)
+        copies.append(copy)
+
+    for m in range(last):
+        start(scaled.at[m], update_hbm.at[m])
+    scale = jnp.broadcast_to(factor[last][:, :1], (TILE, width))
+    for p in range(pieces):
+        for t in range(p * size, (p + 1) * size, TILE):
+            r = slice(t, t + TILE)
+            out[r, :] = scaled[last, r, :] * scale
+        here = pl.ds(p * size, size)
+        start(out.at[here], update_hbm.at[last, here])
+    start(new_rows, rows_hbm)
+    start(new_cols, cols_hbm)
     for copy in copies:
         copy.wait()
 
@@ -549,7 +651,7 @@
         in_specs=[hbm, hbm, hbm],
         out_specs=(vmem, vmem, vmem, vmem),
         scratch_shapes=[
-            pltpu.VMEM((X_SLOTS, 2 * CHUNK, n_col * width), jnp.bfloat16),
+            pltpu.VMEM((X_SLOTS, 2, CHUNK, n_col * width), jnp.bfloat16),
             pltpu.VMEM((S_SLOTS, 2, 4, HALF, RING * width), f32),
             pltpu.VMEM((chunks, 2, 2, HALF, RING * width), f32),
             pltpu.VMEM((chunks, 2, 4, HALF, RING * width), f32),
@@ -565,15 +667,16 @@
             pltpu.VMEM((mats, n_col, rows // LANES, LANES), f32),
             pltpu.VMEM((mats, n_row, 1, width), f32),
             pltpu.VMEM((mats, n_row * n_col, 2, LANES), f32),
-            dma((X_SLOTS,)),
+            dma((X_SLOTS, 2)),
             dma((2,)),
             dma((S_SLOTS, 2)),
             dma((S_SLOTS, 2)),
             dma((S_SLOTS, 2)),
             dma((S_SLOTS, 2)),
-            dma((chunks, 2)),
-            dma((chunks, 2)),
-            dma((chunks, 2)),
+            dma((chunks // mats, 2)),
+            dma((R_SLOTS, 2)),
+            dma((R_SLOTS, 2)),
+            dma((R_SLOTS, 2)),
             dma((chunks, 2)),
             dma((mats, 3)),
             dma((mats, 3)),
@@ -583,13 +686,17 @@
             has_side_effects=True,
             vmem_limit_bytes=50 * 1024 * 1024,
         ),
-    )(grad_terms, row_moment, col_moment)
+    )(
+        grad_terms,
+        pltpu.with_memory_space_constraint(row_moment, pltpu.HBM),
+        pltpu.with_memory_space_constraint(col_moment, pltpu.HBM),
+    )
     return pl.pallas_call(
         finish_kernel,
         out_shape=(shapes[0], shapes[2], shapes[3]),
         in_specs=[vmem] * 4,
         out_specs=(hbm, hbm, hbm),
-        scratch_shapes=[pltpu.VMEM((mats, rows, width), f32), dma((10,))],
+        scratch_shapes=[pltpu.VMEM((rows, width), f32), dma((8,))],
         compiler_params=pltpu.CompilerParams(vmem_limit_bytes=4 * 1024 * 1024),
     )(scaled, factor, new_rows, new_cols)
 

time: 241 us -> 237 us (0.983)
  Pallas kernels: 239 us -> 236 us
    pallas_call x1, Pallas kernels: 237 us -> 234 us  [on_device(): pl.pallas_call(kernel, out_shape=shapes, in_specs=[hbm, hbm, hbm], out_sp...]
where the time goes in v3:
time: 237 us; the launch traced here: 236 us
  Pallas kernels  236 us (100%)
    pallas_call x1, Pallas kernels, on_device(): pl.pallas_call(kernel, out_shape=shapes, in_specs=[hbm, hbm, hbm], out_sp...  234 us

profile of v3, /device:TPU:1, one launch (start us, length us, event | category | flops | bytes accessed | tf_op | source)
XLA Modules:
  0.0 236.4 jit_solution(6333523674259595623)
XLA Ops:
  0.6 234.2 %shard_map.58 = (f32[2,512,640]{2,1,0:T(8,128)S(1)}, f32[2,8,128]{2,1,0:T(8,128)S(1)}, f32[2,512]{1,0:T(2,128)S(1)}, f32[2,640]{1,0:T(2,128)S(1)}) custom-call(bf16[1,2,512,10240]{3,2,1,0:T(8,128)(2,1)} %grad_hbm.1, f32[2,512]{1,0:T(2,128)} %row_hbm.1, f32[2,640]{1,0:T(2,128)} %col_hbm.1), custom_call_target="tpu_custom_call" | custom-call | tf_op jit(solution)/shard_map/pallas_call | solution.py:648
  234.9 1.6 shard_map.59

commit v4 on v3

--- a/solution.py
+++ b/solution.py
@@ -19,7 +19,7 @@
 X_AHEAD = 2
 S_SLOTS = 3
 TILE = 8
-R_SLOTS = 6
+R_SLOTS = 5
 
 second_decay = 1.0 - 100.0 ** (-0.8)
 tiny_square = 1e-30
@@ -81,6 +81,7 @@
     recv2,
     recv3,
     recv4,
+    greet,
     stat_send,
     stat_recv,
 ):
@@ -210,14 +211,9 @@
             send_direct(k, color)
 
     def stage1(k):
-        slot = lax.rem(k, S_SLOTS)
         for color in range(2):
             axis = color
             wait_bytes(land1.at[k, color], recv1.at[lax.rem(k, R_SLOTS), color])
-
-            @pl.when(k >= S_SLOTS)
-            def _():
-                wait_bytes(land1.at[k, color], send1.at[slot, color])
 
             for s in range(RING):
                 top, _ = own(color, k, at(axis, 1), s)
@@ -228,20 +224,15 @@
                 send(
                     land1.at[k, color, which],
                     sum1.at[k, color, which],
-                    send1.at[slot, color],
+                    send1.at[color],
                     recv2.at[lax.rem(k, R_SLOTS), color],
                     neighbour(axis, step),
                 )
 
     def stage2(k):
-        slot = lax.rem(k, S_SLOTS)
         for color in range(2):
             axis = color
             wait_bytes(sum1.at[k, color], recv2.at[lax.rem(k, R_SLOTS), color])
-
-            @pl.when(k >= S_SLOTS)
-            def _():
-                wait_bytes(land2.at[k, color], send2.at[slot, color])
 
             for s in range(RING):
                 top, low = own(color, k, at(axis, 0), s)
@@ -260,38 +251,27 @@
                 send(
                     sum1.at[k, color, which, :, inner_cols(at(axis, 2))],
                     land2.at[k, color, which],
-                    send2.at[slot, color],
+                    send2.at[color],
                     recv3.at[lax.rem(k, R_SLOTS), color],
                     neighbour(axis, step),
                 )
 
     def stage2_direct(k):
-        slot = lax.rem(k, per_mat)
         for color in range(2):
             axis = 1 - color
-
-            @pl.when(k >= per_mat)
-            def _():
-                wait_bytes(land2.at[k, color], send5.at[slot, color])
-
             for half, which, step in ((1, 2, 1), (0, 3, -1)):
                 send(
                     sum1.at[k, color, half, :, inner_cols(at(axis, step))],
                     sum2.at[k, color, which],
-                    send5.at[slot, color],
-                    recv4.at[k, color],
+                    send5.at[color],
+                    recv4.at[k],
                     neighbour(axis, step),
                 )
 
     def stage3(k):
-        slot = lax.rem(k, S_SLOTS)
         for color in range(2):
             axis = 1 - color
             wait_bytes(land2.at[k, color], recv3.at[lax.rem(k, R_SLOTS), color])
-
-            @pl.when(k >= S_SLOTS)
-            def _():
-                wait_bytes(land2.at[k, color], send3.at[slot, color])
 
             for which, step in ((0, 1), (1, -1)):
                 land2[k, color, which] = (
@@ -301,8 +281,8 @@
                 send(
                     land2.at[k, color, which],
                     sum2.at[k, color, which],
-                    send3.at[slot, color],
-                    recv4.at[k, color],
+                    send3.at[color],
+                    recv4.at[k],
                     neighbour(axis, step),
                 )
 
@@ -316,9 +296,9 @@
         m = k // per_mat
         r = lax.rem(k, per_mat) * (2 * CHUNK)
         squares_sum = col_part[m]
+        wait_bytes(sum2.at[k], recv4.at[k])
         for color in range(2):
             axis = 1 - color
-            wait_bytes(sum2.at[k, color], recv4.at[k, color])
             for half, other in ((0, 3), (1, 2)):
                 g = (
                     sum2[k, color, half]
@@ -480,11 +460,14 @@
     row_copy = pltpu.make_async_copy(row_hbm, row_moment, m_sem.at[0])
     col_copy = pltpu.make_async_copy(col_hbm, col_moment, m_sem.at[1])
 
-    def greet_row(d, _):
-        pl.semaphore_signal(
-            barrier, inc=1, device_id=row_peer(d), device_id_type=MESH
-        )
-        return 0
+    near = [t for t in offsets if not any(t[2:])]
+    near = [t for t in near if t in ((1, 0, 0, 0), (n_row0 - 1, 0, 0, 0), (0, 1, 0, 0))]
+
+    def greet_near(sem):
+        for step in near:
+            pl.semaphore_signal(
+                sem, inc=1, device_id=peer(step), device_id_type=MESH
+            )
 
     start_load(0)
     for axis in range(2):
@@ -492,13 +475,13 @@
             pl.semaphore_signal(
                 barrier, inc=1, device_id=neighbour(axis, to), device_id_type=MESH
             )
-    lax.fori_loop(1, n_row, greet_row, 0)
+    greet_near(barrier)
     col_part[...] = jnp.zeros_like(col_part)
     row_copy.start()
     col_copy.start()
     load(0, 0).wait()
     prepare_relay(0, 0)
-    pl.semaphore_wait(barrier, 4 + n_row - 1)
+    pl.semaphore_wait(barrier, 4 + len(near))
     send_relay(0, 0)
     load(0, 1).wait()
     prepare_relay(0, 1)
@@ -508,6 +491,7 @@
     for color in range(2):
         prepare_direct(0, color)
         send_direct(0, color)
+    greet_near(greet.at[0])
     row_copy.wait()
     col_copy.wait()
 
@@ -535,6 +519,15 @@
         @pl.when(it + 1 < chunks)
         def _():
             prepare(it + 1)
+
+        @pl.when(it == 1)
+        def _():
+            pl.semaphore_wait(greet.at[0], len(near))
+            greet_near(greet.at[1])
+
+        @pl.when(it == 2)
+        def _():
+            pl.semaphore_wait(greet.at[1], len(near))
 
         for when, work in (
             (per_mat + 3, early_sums),
@@ -582,22 +575,13 @@
     share_clip(mats - 1)
     finish(mats - 1)
 
-    def drain(slot, _):
-        for color in range(2):
+    for color in range(2):
+        for slot in range(S_SLOTS):
             wait_bytes(stage.at[slot, color], send0.at[slot, color])
-            wait_bytes(land1.at[0, color], send1.at[slot, color])
-            wait_bytes(land2.at[0, color], send2.at[slot, color])
-            wait_bytes(land2.at[0, color], send3.at[slot, color])
-        return 0
-
-    lax.fori_loop(0, S_SLOTS, drain, 0)
-
-    def drain_direct(slot, _):
-        for color in range(2):
-            wait_bytes(land2.at[0, color], send5.at[slot, color])
-        return 0
-
-    lax.fori_loop(0, per_mat, drain_direct, 0)
+        wait_bytes(land1.at[:, color], send1.at[color])
+        wait_bytes(land2.at[:, color], send2.at[color])
+        wait_bytes(land2.at[:, color], send3.at[color])
+        wait_bytes(land2.at[:, color], send5.at[color])
 
 
 def finish_kernel(
@@ -670,14 +654,15 @@
             dma((X_SLOTS, 2)),
             dma((2,)),
             dma((S_SLOTS, 2)),
-            dma((S_SLOTS, 2)),
-            dma((S_SLOTS, 2)),
-            dma((S_SLOTS, 2)),
-            dma((chunks // mats, 2)),
+            dma((2,)),
+            dma((2,)),
+            dma((2,)),
+            dma((2,)),
             dma((R_SLOTS, 2)),
             dma((R_SLOTS, 2)),
             dma((R_SLOTS, 2)),
-            dma((chunks, 2)),
+            dma((chunks,)),
+            pltpu.SemaphoreType.REGULAR((2,)),
             dma((mats, 3)),
             dma((mats, 3)),
         ],

time: 237 us -> 236 us (level)
  no operation moved by 1% of the time
where the time goes in v4:
time: 236 us
  Pallas kernels  235 us (100%)
    pallas_call x1, Pallas kernels, on_device(): pl.pallas_call(kernel, out_shape=shapes, in_specs=[hbm, hbm, hbm], out_sp...  234 us

profile of v4, /device:TPU:1, one launch (start us, length us, event | category | flops | bytes accessed | tf_op | source)
XLA Modules:
  0.0 235.7 jit_solution(11282142684405457775)
XLA Ops:
  0.6 233.5 %shard_map.58 = (f32[2,512,640]{2,1,0:T(8,128)S(1)}, f32[2,8,128]{2,1,0:T(8,128)S(1)}, f32[2,512]{1,0:T(2,128)S(1)}, f32[2,640]{1,0:T(2,128)S(1)}) custom-call(bf16[1,2,512,10240]{3,2,1,0:T(8,128)(2,1)} %grad_hbm.1, f32[2,512]{1,0:T(2,128)} %row_hbm.1, f32[2,640]{1,0:T(2,128)} %col_hbm.1), custom_call_target="tpu_custom_call" | custom-call | tf_op jit(solution)/shard_map/pallas_call | solution.py:632
  234.2 1.6 shard_map.59

commit v5 on v4

--- a/solution.py
+++ b/solution.py
@@ -70,6 +70,8 @@
     row_land,
     col_land,
     all_land,
+    late_land,
+    late_all,
     x_sem,
     m_sem,
     send0,
@@ -325,15 +327,15 @@
             def _():
                 ref[i : i + 1, lanes] = value
 
+    lane = lax.broadcasted_iota(jnp.int32, (1, LANES), 1)
+    is_early = lane < LANES - 2 * CHUNK
+    assert 2 * CHUNK == LANES // 2
+
     def lane_major(part):
         return jnp.sum(part.T, axis=0, keepdims=True)
 
     def group(b):
         return slice(b * LANES, (b + 1) * LANES)
-
-    def early_sums(m):
-        for b in range(row_groups - 1):
-            row_land[m, my_col, b : b + 1, :] = lane_major(row_part[m, group(b), :])
 
     def peer(step):
         z, core, x, y = step
@@ -346,24 +348,27 @@
             there["col_1"] = at(1, y)
         return there
 
+    def to_cols(m, buf, which):
+        mine = buf.at[m, my_col]
+        for step in offsets:
+            if not any(step[:2]):
+                send(
+                    mine, mine, stat_send.at[m, which], stat_recv.at[m, which], peer(step)
+                )
+
+    def share_early(m):
+        for b in range(row_groups):
+            row_land[m, my_col, b : b + 1, :] = lane_major(row_part[m, group(b), :])
+        to_cols(m, row_land, 1)
+
     def share_sums(m):
         col_land[m, my_row] = jnp.sum(col_part[m], axis=0, keepdims=True)
         mine = col_land.at[m, my_row]
         for step in offsets:
             if not any(step[2:]):
                 send(mine, mine, stat_send.at[m, 0], stat_recv.at[m, 0], peer(step))
-        b = row_groups - 1
-        row_land[m, my_col, b : b + 1, :] = lane_major(row_part[m, group(b), :])
-        rows_mine = row_land.at[m, my_col]
-        for step in offsets:
-            if not any(step[:2]):
-                send(
-                    rows_mine,
-                    rows_mine,
-                    stat_send.at[m, 1],
-                    stat_recv.at[m, 1],
-                    peer(step),
-                )
+        late_land[m, my_col] = lane_major(row_part[m, group(row_groups - 1), :])
+        to_cols(m, late_land, 3)
 
     def all_but_one(m, buf, sem, n):
         if n > 1:
@@ -400,21 +405,28 @@
                 second_decay * pick(row_moment, m, group(b))
                 + (1.0 - second_decay) * full[b : b + 1] / total_cols
             )
+            moments.append(moment)
             part = weighted_row[b : b + 1, :] / moment
+            if b == row_groups - 1:
+                part = jnp.where(is_early, part, 0.0)
+                moment = jnp.where(is_early, moment, 0.0)
             clip = part if clip is None else clip + part
             level = moment if level is None else level + moment
-            moments.append(moment)
-        all_land[m, me, 0:1, :] = clip
-        all_land[m, me, 1:2, :] = level
+        clip = clip + pltpu.roll(clip, LANES // 2, 1)
+        level = level + pltpu.roll(level, LANES // 2, 1)
+        late = (
+            second_decay * pick(row_moment, m, group(row_groups - 1)) / n_col
+            + (1.0 - second_decay) * late_land[m, my_col] / total_cols
+        )
+        late_weight = pltpu.roll(
+            weighted_row[row_groups - 1 : row_groups, :], LANES // 2, 1
+        )
+        all_land[m, me, 0:1, :] = jnp.where(is_early, clip, level)
+        all_land[m, me, 1:2, :] = jnp.where(is_early, late_weight, late)
         mine = all_land.at[m, me]
         for step in offsets:
             send(mine, mine, stat_send.at[m, 2], stat_recv.at[m, 2], peer(step))
         put(new_cols, m, slice(None), col)
-        for b in range(row_groups):
-            put(new_rows, m, group(b), moments[b])
-            row_scale[group(b), :] = jnp.broadcast_to(
-                lax.rsqrt(moments[b]), (LANES, LANES)
-            ).T
         col_scale = jnp.broadcast_to(lax.rsqrt(col), (TILE, width))
 
         def rescale(t, _):
@@ -425,16 +437,46 @@
                 update[m, r, lanes] = update[m, r, lanes] * col_scale[:, lanes] * scale
             return 0
 
-        lax.fori_loop(0, rows // TILE, rescale, 0, unroll=8)
+        for b in range(row_groups - 1):
+            put(new_rows, m, group(b), moments[b])
+            row_scale[group(b), :] = jnp.broadcast_to(
+                lax.rsqrt(moments[b]), (LANES, LANES)
+            ).T
+        tiles = (row_groups - 1) * LANES // TILE
+        lax.fori_loop(0, tiles, rescale, 0, unroll=8)
+
+        all_but_one(m, late_land, stat_recv.at[m, 3], n_col)
+        full = late_land[m, 0]
+        for s in range(1, n_col):
+            full = full + late_land[m, s]
+        b = row_groups - 1
+        moment = (
+            second_decay * pick(row_moment, m, group(b))
+            + (1.0 - second_decay) * full / total_cols
+        )
+        moment = jnp.where(is_early, moments[b], moment)
+        put(new_rows, m, group(b), moment)
+        row_scale[group(b), :] = jnp.broadcast_to(lax.rsqrt(moment), (LANES, LANES)).T
+        lax.fori_loop(tiles, rows // TILE, rescale, 0, unroll=8)
 
     def finish(m):
         all_but_one(m, all_land, stat_recv.at[m, 2], n_row * n_col)
-        parts = [all_land[m, s] for s in range(4)]
-        for s in range(4, n_row * n_col):
-            parts[s % 4] = parts[s % 4] + all_land[m, s]
-        total = (parts[0] + parts[1]) + (parts[2] + parts[3])
-        level = jnp.sum(total[1:2], axis=1, keepdims=True) / (n_col * total_rows)
-        clip = jnp.sum(total[0:1], axis=1, keepdims=True)
+        total = None
+        for r in range(n_row):
+            parts = [all_land[m, r * n_col + c] for c in range(4)]
+            for c in range(4, n_col):
+                parts[c % 4] = parts[c % 4] + all_land[m, r * n_col + c]
+            one_row = (parts[0] + parts[1]) + (parts[2] + parts[3])
+            total = one_row if total is None else total + one_row
+            late_all[r : r + 1, :] = one_row[1:2]
+        late = late_all[...]
+        ratio = late / pltpu.roll(late, LANES // 2, 1)
+        clip = jnp.where(is_early, total[0:1], 0.0) + jnp.sum(
+            jnp.where(is_early, ratio, 0.0), axis=0, keepdims=True
+        )
+        level = jnp.where(is_early, 0.0, total[0:1] / n_col + total[1:2])
+        clip = jnp.sum(clip, axis=1, keepdims=True)
+        level = jnp.sum(level, axis=1, keepdims=True) / total_rows
         clip_scale = jnp.maximum(
             1.0, jnp.sqrt(clip * level / (total_rows * total_cols))
         )
@@ -455,6 +497,7 @@
         all_but_one(m, col_land, stat_send.at[m, 0], n_row)
         all_but_one(m, row_land, stat_send.at[m, 1], n_col)
         all_but_one(m, all_land, stat_send.at[m, 2], n_row * n_col)
+        all_but_one(m, late_land, stat_send.at[m, 3], n_col)
 
     barrier = pltpu.get_barrier_semaphore()
     row_copy = pltpu.make_async_copy(row_hbm, row_moment, m_sem.at[0])
@@ -477,6 +520,9 @@
             )
     greet_near(barrier)
     col_part[...] = jnp.zeros_like(col_part)
+    row_part[:, rows - 2 * CHUNK :, :] = jnp.zeros(
+        (mats, 2 * CHUNK, LANES), jnp.float32
+    )
     row_copy.start()
     col_copy.start()
     load(0, 0).wait()
@@ -530,7 +576,7 @@
             pl.semaphore_wait(greet.at[1], len(near))
 
         for when, work in (
-            (per_mat + 3, early_sums),
+            (per_mat + 3, share_early),
             (per_mat + 3, share_sums),
             (per_mat + 5, share_clip),
             (per_mat + 7, finish),
@@ -569,7 +615,7 @@
         return 0
 
     lax.fori_loop(per_mat, last, finish_chunk, 0)
-    early_sums(mats - 1)
+    share_early(mats - 1)
     stage4(last)
     share_sums(mats - 1)
     share_clip(mats - 1)
@@ -651,6 +697,8 @@
             pltpu.VMEM((mats, n_col, rows // LANES, LANES), f32),
             pltpu.VMEM((mats, n_row, 1, width), f32),
             pltpu.VMEM((mats, n_row * n_col, 2, LANES), f32),
+            pltpu.VMEM((mats, n_col, 1, LANES), f32),
+            pltpu.VMEM((n_row, LANES), f32),
             dma((X_SLOTS, 2)),
             dma((2,)),
             dma((S_SLOTS, 2)),
@@ -663,8 +711,8 @@
             dma((R_SLOTS, 2)),
             dma((chunks,)),
             pltpu.SemaphoreType.REGULAR((2,)),
-            dma((mats, 3)),
-            dma((mats, 3)),
+            dma((mats, 4)),
+            dma((mats, 4)),
         ],
         compiler_params=pltpu.CompilerParams(
             collective_id=0,

time: 236 us -> 235 us (level)
  no operation moved by 1% of the time
where the time goes in v5:
time: 235 us
  Pallas kernels  234 us (100%)
    pallas_call x1, Pallas kernels, on_device(): pl.pallas_call(kernel, out_shape=shapes, in_specs=[hbm, hbm, hbm], out_sp...  233 us

profile of v5, /device:TPU:1, one launch (start us, length us, event | category | flops | bytes accessed | tf_op | source)
XLA Modules:
  0.0 235.1 jit_solution(5525515483211590579)
XLA Ops:
  0.6 232.9 %shard_map.58 = (f32[2,512,640]{2,1,0:T(8,128)S(1)}, f32[2,8,128]{2,1,0:T(8,128)S(1)}, f32[2,512]{1,0:T(2,128)S(1)}, f32[2,640]{1,0:T(2,128)S(1)}) custom-call(bf16[1,2,512,10240]{3,2,1,0:T(8,128)(2,1)} %grad_hbm.1, f32[2,512]{1,0:T(2,128)} %row_hbm.1, f32[2,640]{1,0:T(2,128)} %col_hbm.1), custom_call_target="tpu_custom_call" | custom-call | tf_op jit(solution)/shard_map/pallas_call | solution.py:678
  233.5 1.6 shard_map.59

commit v6 on v5

--- a/solution.py
+++ b/solution.py
@@ -129,19 +129,19 @@
             device_id_type=MESH,
         ).start()
 
-    def load(k, color):
+    def load(k, color, sem):
         slot = lax.rem(k, X_SLOTS)
         m = k // per_mat
         r = lax.rem(k, per_mat) * (2 * CHUNK) + color * CHUNK
         return pltpu.make_async_copy(
             grad_hbm.at[0, m, pl.ds(pl.multiple_of(r, CHUNK), CHUNK), :],
             x_in.at[slot, color],
-            x_sem.at[slot, color],
+            sem,
         )
 
     def start_load(k):
         for color in range(2):
-            load(k, color).start()
+            load(k, color, x_sem.at[lax.rem(k, X_SLOTS)]).start()
 
     def own(color, k, idx, seg):
         outer, inner = (idx, seg) if color == 0 else (seg, idx)
@@ -155,12 +155,12 @@
     def inner_cols(idx):
         return pl.ds(pl.multiple_of(idx * width, LANES), width)
 
-    def free_stage(k, color):
+    def free_stage(k):
         slot = lax.rem(k, S_SLOTS)
 
         @pl.when(k >= S_SLOTS)
         def _():
-            wait_bytes(stage.at[slot, color], send0.at[slot, color])
+            wait_bytes(stage.at[slot], send0.at[slot])
 
     def prepare_relay(k, color):
         slot = lax.rem(k, S_SLOTS)
@@ -178,9 +178,10 @@
             stage[slot, color, 3, :, cols(s)] = top
 
     def prepare(k):
-        for color in range(2):
-            load(k, color).wait()
-            free_stage(k, color)
+        slot = lax.rem(k, X_SLOTS)
+        wait_bytes(x_in.at[slot], x_sem.at[slot])
+        free_stage(k)
+        for color in range(2):
             prepare_relay(k, color)
             prepare_direct(k, color)
 
@@ -190,8 +191,8 @@
             send(
                 stage.at[slot, color, which],
                 land1.at[k, color, which],
-                send0.at[slot, color],
-                recv1.at[lax.rem(k, R_SLOTS), color],
+                send0.at[slot],
+                recv1.at[lax.rem(k, R_SLOTS)],
                 neighbour(color, step),
             )
 
@@ -201,8 +202,8 @@
             send(
                 stage.at[slot, color, which],
                 sum1.at[k, color, which],
-                send0.at[slot, color],
-                recv2.at[lax.rem(k, R_SLOTS), color],
+                send0.at[slot],
+                recv2.at[lax.rem(k, R_SLOTS)],
                 neighbour(color, step),
             )
 
@@ -213,9 +214,9 @@
             send_direct(k, color)
 
     def stage1(k):
+        wait_bytes(land1.at[k], recv1.at[lax.rem(k, R_SLOTS)])
         for color in range(2):
             axis = color
-            wait_bytes(land1.at[k, color], recv1.at[lax.rem(k, R_SLOTS), color])
 
             for s in range(RING):
                 top, _ = own(color, k, at(axis, 1), s)
@@ -226,15 +227,15 @@
                 send(
                     land1.at[k, color, which],
                     sum1.at[k, color, which],
-                    send1.at[color],
-                    recv2.at[lax.rem(k, R_SLOTS), color],
+                    send1.at[0],
+                    recv2.at[lax.rem(k, R_SLOTS)],
                     neighbour(axis, step),
                 )
 
     def stage2(k):
+        wait_bytes(sum1.at[k], recv2.at[lax.rem(k, R_SLOTS)])
         for color in range(2):
             axis = color
-            wait_bytes(sum1.at[k, color], recv2.at[lax.rem(k, R_SLOTS), color])
 
             for s in range(RING):
                 top, low = own(color, k, at(axis, 0), s)
@@ -253,8 +254,8 @@
                 send(
                     sum1.at[k, color, which, :, inner_cols(at(axis, 2))],
                     land2.at[k, color, which],
-                    send2.at[color],
-                    recv3.at[lax.rem(k, R_SLOTS), color],
+                    send2.at[0],
+                    recv3.at[lax.rem(k, R_SLOTS)],
                     neighbour(axis, step),
                 )
 
@@ -265,15 +266,15 @@
                 send(
                     sum1.at[k, color, half, :, inner_cols(at(axis, step))],
                     sum2.at[k, color, which],
-                    send5.at[color],
+                    send5.at[0],
                     recv4.at[k],
                     neighbour(axis, step),
                 )
 
     def stage3(k):
+        wait_bytes(land2.at[k], recv3.at[lax.rem(k, R_SLOTS)])
         for color in range(2):
             axis = 1 - color
-            wait_bytes(land2.at[k, color], recv3.at[lax.rem(k, R_SLOTS), color])
 
             for which, step in ((0, 1), (1, -1)):
                 land2[k, color, which] = (
@@ -283,7 +284,7 @@
                 send(
                     land2.at[k, color, which],
                     sum2.at[k, color, which],
-                    send3.at[color],
+                    send3.at[0],
                     recv4.at[k],
                     neighbour(axis, step),
                 )
@@ -353,7 +354,7 @@
         for step in offsets:
             if not any(step[:2]):
                 send(
-                    mine, mine, stat_send.at[m, which], stat_recv.at[m, which], peer(step)
+                    mine, mine, stat_send.at[which], stat_recv.at[m, which], peer(step)
                 )
 
     def share_early(m):
@@ -366,7 +367,7 @@
         mine = col_land.at[m, my_row]
         for step in offsets:
             if not any(step[2:]):
-                send(mine, mine, stat_send.at[m, 0], stat_recv.at[m, 0], peer(step))
+                send(mine, mine, stat_send.at[0], stat_recv.at[m, 0], peer(step))
         late_land[m, my_col] = lane_major(row_part[m, group(row_groups - 1), :])
         to_cols(m, late_land, 3)
 
@@ -425,7 +426,7 @@
         all_land[m, me, 1:2, :] = jnp.where(is_early, late_weight, late)
         mine = all_land.at[m, me]
         for step in offsets:
-            send(mine, mine, stat_send.at[m, 2], stat_recv.at[m, 2], peer(step))
+            send(mine, mine, stat_send.at[2], stat_recv.at[m, 2], peer(step))
         put(new_cols, m, slice(None), col)
         col_scale = jnp.broadcast_to(lax.rsqrt(col), (TILE, width))
 
@@ -494,10 +495,10 @@
 
             lax.fori_loop(0, rows // TILE, one, 0, unroll=4)
 
-        all_but_one(m, col_land, stat_send.at[m, 0], n_row)
-        all_but_one(m, row_land, stat_send.at[m, 1], n_col)
-        all_but_one(m, all_land, stat_send.at[m, 2], n_row * n_col)
-        all_but_one(m, late_land, stat_send.at[m, 3], n_col)
+        all_but_one(m, col_land, stat_send.at[0], n_row)
+        all_but_one(m, row_land, stat_send.at[1], n_col)
+        all_but_one(m, all_land, stat_send.at[2], n_row * n_col)
+        all_but_one(m, late_land, stat_send.at[3], n_col)
 
     barrier = pltpu.get_barrier_semaphore()
     row_copy = pltpu.make_async_copy(row_hbm, row_moment, m_sem.at[0])
@@ -512,7 +513,9 @@
                 sem, inc=1, device_id=peer(step), device_id_type=MESH
             )
 
-    start_load(0)
+    first = [load(0, color, m_sem.at[2 + color]) for color in range(2)]
+    for copy in first:
+        copy.start()
     for axis in range(2):
         for to in (1, -1):
             pl.semaphore_signal(
@@ -525,11 +528,11 @@
     )
     row_copy.start()
     col_copy.start()
-    load(0, 0).wait()
+    first[0].wait()
     prepare_relay(0, 0)
     pl.semaphore_wait(barrier, 4 + len(near))
     send_relay(0, 0)
-    load(0, 1).wait()
+    first[1].wait()
     prepare_relay(0, 1)
     send_relay(0, 1)
     for k in range(1, 1 + X_AHEAD):
@@ -621,13 +624,12 @@
     share_clip(mats - 1)
     finish(mats - 1)
 
-    for color in range(2):
-        for slot in range(S_SLOTS):
-            wait_bytes(stage.at[slot, color], send0.at[slot, color])
-        wait_bytes(land1.at[:, color], send1.at[color])
-        wait_bytes(land2.at[:, color], send2.at[color])
-        wait_bytes(land2.at[:, color], send3.at[color])
-        wait_bytes(land2.at[:, color], send5.at[color])
+    for slot in range(S_SLOTS):
+        wait_bytes(stage.at[slot], send0.at[slot])
+    wait_bytes(land1, send1.at[0])
+    wait_bytes(land2, send2.at[0])
+    wait_bytes(land2, send3.at[0])
+    wait_bytes(land2, send5.at[0])
 
 
 def finish_kernel(
@@ -699,19 +701,19 @@
             pltpu.VMEM((mats, n_row * n_col, 2, LANES), f32),
             pltpu.VMEM((mats, n_col, 1, LANES), f32),
             pltpu.VMEM((n_row, LANES), f32),
-            dma((X_SLOTS, 2)),
-            dma((2,)),
-            dma((S_SLOTS, 2)),
-            dma((2,)),
-            dma((2,)),
-            dma((2,)),
-            dma((2,)),
-            dma((R_SLOTS, 2)),
-            dma((R_SLOTS, 2)),
-            dma((R_SLOTS, 2)),
+            dma((X_SLOTS,)),
+            dma((4,)),
+            dma((S_SLOTS,)),
+            dma((1,)),
+            dma((1,)),
+            dma((1,)),
+            dma((1,)),
+            dma((R_SLOTS,)),
+            dma((R_SLOTS,)),
+            dma((R_SLOTS,)),
             dma((chunks,)),
             pltpu.SemaphoreType.REGULAR((2,)),
-            dma((mats, 4)),
+            dma((4,)),
             dma((mats, 4)),
         ],
         compiler_params=pltpu.CompilerParams(

time: 235 us -> 235 us (level)
  no operation moved by 1% of the time
where the time goes in v6:
time: 235 us
  Pallas kernels  234 us (100%)
    pallas_call x1, Pallas kernels, on_device(): pl.pallas_call(kernel, out_shape=shapes, in_specs=[hbm, hbm, hbm], out_sp...  233 us

profile of v6, /device:TPU:1, one launch (start us, length us, event | category | flops | bytes accessed | tf_op | source)
XLA Modules:
  0.0 234.8 jit_solution(17165916052300471346)
XLA Ops:
  0.6 232.6 %shard_map.58 = (f32[2,512,640]{2,1,0:T(8,128)S(1)}, f32[2,8,128]{2,1,0:T(8,128)S(1)}, f32[2,512]{1,0:T(2,128)S(1)}, f32[2,640]{1,0:T(2,128)S(1)}) custom-call(bf16[1,2,512,10240]{3,2,1,0:T(8,128)(2,1)} %grad_hbm.1, f32[2,512]{1,0:T(2,128)} %row_hbm.1, f32[2,640]{1,0:T(2,128)} %col_hbm.1), custom_call_target="tpu_custom_call" | custom-call | tf_op jit(solution)/shard_map/pallas_call | solution.py:680
  233.3 1.6 shard_map.59

commit v7 on v6

--- a/solution.py
+++ b/solution.py
@@ -267,7 +267,7 @@
                     sum1.at[k, color, half, :, inner_cols(at(axis, step))],
                     sum2.at[k, color, which],
                     send5.at[0],
-                    recv4.at[k],
+                    recv4.at[lax.rem(k, per_mat)],
                     neighbour(axis, step),
                 )
 
@@ -285,7 +285,7 @@
                     land2.at[k, color, which],
                     sum2.at[k, color, which],
                     send3.at[0],
-                    recv4.at[k],
+                    recv4.at[lax.rem(k, per_mat)],
                     neighbour(axis, step),
                 )
 
@@ -299,7 +299,7 @@
         m = k // per_mat
         r = lax.rem(k, per_mat) * (2 * CHUNK)
         squares_sum = col_part[m]
-        wait_bytes(sum2.at[k], recv4.at[k])
+        wait_bytes(sum2.at[k], recv4.at[lax.rem(k, per_mat)])
         for color in range(2):
             axis = 1 - color
             for half, other in ((0, 3), (1, 2)):
@@ -711,7 +711,7 @@
             dma((R_SLOTS,)),
             dma((R_SLOTS,)),
             dma((R_SLOTS,)),
-            dma((chunks,)),
+            dma((chunks // mats,)),
             pltpu.SemaphoreType.REGULAR((2,)),
             dma((4,)),
             dma((mats, 4)),

time: 235 us -> 235 us (level)
  no operation moved by 1% of the time
where the time goes in v7:
time: 235 us
  Pallas kernels  234 us (100%)
    pallas_call x1, Pallas kernels, on_device(): pl.pallas_call(kernel, out_shape=shapes, in_specs=[hbm, hbm, hbm], out_sp...  233 us

profile of v7, /device:TPU:1, one launch (start us, length us, event | category | flops | bytes accessed | tf_op | source)
XLA Modules:
  0.0 234.8 jit_solution(6836071027289420883)
XLA Ops:
  0.6 232.6 %shard_map.58 = (f32[2,512,640]{2,1,0:T(8,128)S(1)}, f32[2,8,128]{2,1,0:T(8,128)S(1)}, f32[2,512]{1,0:T(2,128)S(1)}, f32[2,640]{1,0:T(2,128)S(1)}) custom-call(bf16[1,2,512,10240]{3,2,1,0:T(8,128)(2,1)} %grad_hbm.1, f32[2,512]{1,0:T(2,128)} %row_hbm.1, f32[2,640]{1,0:T(2,128)} %col_hbm.1), custom_call_target="tpu_custom_call" | custom-call | tf_op jit(solution)/shard_map/pallas_call | solution.py:680
  233.2 1.6 shard_map.59
